TPU v7x, 32 devices: a whole 2x2x4 slice. The times are simulated.
32 devices in a mesh: dp: 2 (over core), expert: 4 (over y, x), mp: 4 (over z).
Axes of the slice: x: 2, y: 2, z: 4, core: 2. Of those that a mesh axis runs over, the one named last changes fastest.
Arguments:
- hidden: bfloat16 [3072, 2, 7168], P(('dp', 'expert'), None, 'mp'), may hold values from -6 to 6
- cotangent: bfloat16 [3072, 2048], P(('dp', 'expert'), 'mp'), may hold values from -6 to 6
- routes: int32 [3072, 2], P(('dp', 'expert')), may hold values from 0 to 3, all different within a row; in each aligned block of 384 rows (0 to 383, 384 to 767, ...) at most 288 rows name the same one
- combine: float32 [3072, 2], P(('dp', 'expert')), may hold values from 0.1 to 0.9
- block_pair: int32 [8, 12], P(('dp', 'expert')), may hold values from 0 to 11, each once within a row
- lengths: int32 [8, 12], P(('dp', 'expert')), may hold values from 4 to 32
- log_ratio: float32 [8, 12], P(('dp', 'expert')), may hold values from -30 to 30
Outputs:
- grad_down: float32 [4, 7168, 2048], P('expert', ('mp', 'dp'))
- expert_load: float32 [4], replicated
Inputs may be any that keep to these rules, and one draw needn't show every extreme that they name: `routes`: each row names 2 different experts; in each aligned block of 384 rows (the rows of one device) no expert is named more than 288 times, and in some blocks one expert is named exactly 288 times. `block_pair`: each row holds every number of 0 to 11 once; value v marks the chosen response of the row's pair v // 2 if v is even, its rejected response if v is odd.
All inputs are finite; a program needn't handle non-finite values.
Results may differ from a plain program's by a relative error of at most 0.0029.
Values may be sent and summed in bfloat16 or wider, within the bound.
No kernel may reach another device: no remote copies, remote signals or barrier semaphores. Data moves between devices by JAX's collectives and lax.ppermute only.
A program may use at most 128 MiB of HBM per device.

v0:
```python
import functools
import math
import jax
import jax.numpy as jnp
from jax import lax
from jax.experimental import pallas as pl
from jax.experimental.pallas import tpu as pltpu
from jax.sharding import PartitionSpec as P


BETA = 0.1
F32 = jnp.float32
BF16 = jnp.bfloat16
VM = pl.BlockSpec(memory_space=pltpu.VMEM)
ANY = pl.BlockSpec(memory_space=pl.ANY)
HBM = pl.BlockSpec(memory_space=pltpu.HBM)


def iota(shape, dim):
    return lax.broadcasted_iota(jnp.int32, shape, dim)


def other(place, hop, size):
    return place ^ hop if size & (size - 1) == 0 else lax.rem(place + hop, size)


def pairs_of(size, hop):
    return [(i, i ^ hop if size & (size - 1) == 0 else (i + hop) % size) for i in range(size)]


def pack_scaled(groups, most, early, *refs):
    load, ranks, shares, routes, raw = refs[6:11]
    scaled = refs[11 : 11 + groups]
    combine, pair, lengths, ratio, cot, sem = refs[11 + groups :]
    copies = [
        pltpu.make_async_copy(source, held, sem.at[i])
        for i, (source, held) in enumerate(zip(refs[:6], (routes, combine, pair, lengths, ratio, cot)))
    ]
    for copy in copies:
        copy.start()
    for copy in copies:
        copy.wait()
    blocks = pair.shape[1]
    rows = routes.shape[1]
    length = rows // blocks
    pair_row = jnp.broadcast_to(pair[...], (blocks, blocks))
    ratio_row = jnp.broadcast_to(ratio[...], (blocks, blocks))
    length_row = jnp.broadcast_to(lengths[...], (blocks, blocks))
    eye = iota((blocks, blocks), 0) == iota((blocks, blocks), 1)
    pair_col = jnp.sum(jnp.where(eye, pair_row, 0), axis=1, keepdims=True)
    length_col = jnp.sum(jnp.where(eye, length_row, 0), axis=1, keepdims=True)
    chosen = jnp.sum(jnp.where(pair_row == (pair_col & -2), ratio_row, 0.0), axis=1, keepdims=True)
    refused = jnp.sum(jnp.where(pair_row == (pair_col | 1), ratio_row, 0.0), axis=1, keepdims=True)
    coef = BETA * jax.nn.sigmoid(-BETA * (chosen - refused))
    block_weight = jnp.where((pair_col & 1) == 0, -coef, coef)
    owner = iota((blocks, rows), 1) // length == iota((blocks, rows), 0)
    weight = jnp.sum(jnp.where(owner, block_weight, 0.0), axis=0, keepdims=True)
    valid = jnp.sum(jnp.where(owner, length_col, 0), axis=0, keepdims=True)
    live = iota((1, rows), 1) % length < valid
    weight = jnp.where(live, weight, 0.0)
    first, second = routes[0:1, :], routes[1:2, :]
    weight0, weight1 = combine[0:1, :] * weight, combine[1:2, :] * weight
    pad = -(-groups // 8) * 8
    label = iota((pad, rows), 0)
    counted = ((first == label) | (second == label)) & live
    counts = jnp.sum(jnp.where(counted, 1.0, 0.0), axis=1, keepdims=True)
    load[...] = jnp.broadcast_to(counts, load.shape)
    named = other(jnp.full((pad, rows), lax.axis_index("expert"), jnp.int32), label, groups)
    hit0, hit1 = first == named, second == named
    hit = hit0 | hit1
    before = jnp.where(iota((rows, rows), 0) < iota((rows, rows), 1), 1.0, 0.0).astype(BF16)
    rank = jnp.dot(jnp.where(hit, 1.0, 0.0).astype(BF16), before, preferred_element_type=F32)
    key = jnp.where(hit, rank, -1.0)
    by_group = jnp.where(hit0, weight0, jnp.where(hit1, weight1, 0.0))
    ranks[...] = key
    shares[...] = by_group
    raw[...] = cot[:, : raw.shape[1]]
    place_scaled(most, key, by_group, cot[:, early:], scaled)


def place_scaled(most, key, by_group, source, outs):
    slot = iota((most, key.shape[1]), 0).astype(F32)
    for j, out in enumerate(outs):
        at = slot == key[j : j + 1, :]
        row_weight = jnp.sum(jnp.where(at, by_group[j : j + 1, :], 0.0), axis=1, keepdims=True)
        taken = jnp.dot(jnp.where(at, 1.0, 0.0).astype(BF16), source, preferred_element_type=F32)
        out[:most, :] = (row_weight * taken).astype(BF16)


def pack_early(most, line, key, by_group, load, *refs):
    source, outs = jnp.concatenate([x[...] for x in refs[:line]], axis=1), refs[line:]
    place_scaled(most, key[...], by_group[...], source, outs)
    counts = split_counts(load[:, :1], source.shape[1])
    for out in outs:
        out[most:, :] = counts


def split_counts(counts, columns):
    high = jnp.floor(counts * (1.0 / 128.0))
    both = jnp.concatenate([high, counts - 128.0 * high], axis=0)
    return jnp.broadcast_to(both, (both.shape[0], columns)).astype(BF16)


def read_counts(rows):
    rows = rows.astype(F32)
    half = rows.shape[0] // 2
    return 128.0 * rows[:half] + rows[half:]


def join_early(most, *refs):
    blocks, out = refs[:-1], refs[-1]
    counts = sum(read_counts(block[most:, :128]) for block in blocks)
    for i, block in enumerate(blocks):
        out[i * most : (i + 1) * most, :] = block[:most, :]
    out[len(blocks) * most :, :] = split_counts(counts[:, :1], out.shape[1])


def tally(rows, mine, theirs, out):
    out[...] = read_counts(mine[rows:, :128]) + read_counts(theirs[rows:, :128])


def pack_hidden(groups, most, hop, halves, routes, key, hidden, *outs):
    rows, top, inner = hidden.shape
    width = inner // halves
    flat = rows * top
    part = other(lax.axis_index("dp"), hop, halves) if halves > 1 else 0
    columns = pl.ds(pl.multiple_of(part * width, 128), width)
    pad = key.shape[0]
    spread = jnp.where(iota((rows, flat), 0) == iota((rows, flat), 1) // top, 1.0, 0.0).astype(BF16)
    high = jnp.floor(key[...] * (1.0 / 16.0))
    low = key[...] - 16.0 * high
    named = [jnp.broadcast_to(routes[k : k + 1, :].astype(F32), (pad, rows)) for k in range(top)]
    stacked = jnp.concatenate([high, low] + named, axis=0).astype(BF16)
    wide = jnp.dot(stacked, spread, preferred_element_type=F32)
    key = 16.0 * wide[:pad] + wide[pad : 2 * pad]
    choice = iota((pad, flat), 1) % top
    route = wide[2 * pad : 3 * pad]
    for k in range(1, top):
        route = jnp.where(choice == k, wide[(2 + k) * pad : (3 + k) * pad], route)
    me = jnp.full((pad, flat), lax.axis_index("expert"), jnp.int32)
    label = other(me, iota((pad, flat), 0), groups).astype(F32)
    key = jnp.where(route == label, key, -1.0)
    slot = iota((most, flat), 0).astype(F32)
    source = hidden[:, :, columns].reshape(flat, width)
    for j in range(groups):
        at = jnp.where(slot == key[j : j + 1, :], 1.0, 0.0).astype(BF16)
        outs[j][...] = jnp.dot(at, source, preferred_element_type=F32).astype(BF16)


def turn(step, *refs):
    blocks, out, joined = refs[:-2], refs[-2], refs[-1]
    most = blocks[0].shape[0]
    for i, block in enumerate(blocks):
        joined[i * most : (i + 1) * most, :] = block[...]
    for i in range(0, joined.shape[0], step):
        out[:, i : i + step] = joined[i : i + step, :].T


def stack_into(out, parts):
    at = 0
    for part in parts:
        out[at : at + part.shape[0], :] = part[...]
        at += part.shape[0]


def join(*refs):
    stack_into(refs[-1], refs[:-1])


def join_either(hop, *refs):
    half = (len(refs) - 1) // 2
    from_below = lax.axis_index("mp") >= hop

    @pl.when(from_below)
    def _():
        stack_into(refs[-1], refs[:half])

    @pl.when(jnp.logical_not(from_below))
    def _():
        stack_into(refs[-1], refs[half:-1])


def arrival(which, hop, line):
    m = lax.axis_index("mp")
    low, high = m >= hop, m + hop < line
    if which == "below":
        return low, m - hop
    if which == "above":
        return high, m + hop
    return low | high, jnp.where(low, m - hop, m + hop)


def half_product(tile, ht, mine, out):
    for i in range(0, ht.shape[0], tile):
        out[i : i + tile, :] = jnp.dot(
            ht[i : i + tile, : mine.shape[0]], mine[...], preferred_element_type=F32
        )


def last_product(tile, line, which, hop, ht, first, theirs, _, out, total, sem):
    rows, width = theirs.shape
    shard = out.shape[1] // line
    valid, at = arrival(which, hop, line)

    @pl.when(valid)
    def _():
        column = pl.multiple_of(at * shard + shard - width, 128)
        copies = []
        for i in range(0, ht.shape[0], tile):
            total[i : i + tile, :] = first[i : i + tile, :] + jnp.dot(
                ht[i : i + tile, rows:], theirs[...], preferred_element_type=F32
            )
            copy = pltpu.make_async_copy(
                total.at[pl.ds(i, tile)],
                out.at[pl.ds(i, tile), pl.ds(column, width)],
                sem.at[i // tile],
            )
            copy.start()
            copies.append(copy)
        for copy in copies:
            copy.wait()


def product(tile, line, steps, ht, *refs):
    sources, (out, joined, total, sem) = refs[: 2 * max(len(steps), 1)], refs[-4:]
    rows, width = ht.shape[1] // 2, sources[0].shape[1]
    shard = out.shape[1] // line
    for k in range(len(sources)):
        at = (k % 2) * rows, (k // 2) * width
        joined[at[0] : at[0] + rows, at[1] : at[1] + width] = sources[k][:rows, :]
    if steps:
        marks = [arrival(which, hop, line) for which, hop in steps]
        marks = [(valid, at * shard + shard - width, width) for valid, at in marks]
    else:
        m = lax.axis_index("mp")
        marks = [(m >= 0, lax.rem(m + line - k, line) * shard, width // line) for k in range(line)]
    tiles = ht.shape[0] // tile

    def write(i, k, act):
        valid, column, size = marks[k]

        @pl.when(valid)
        def _():
            act(
                pltpu.make_async_copy(
                    total.at[pl.ds(i * tile, tile), pl.ds(k * size, size)],
                    out.at[pl.ds(i * tile, tile), pl.ds(pl.multiple_of(column, 128), size)],
                    sem.at[i * len(marks) + k],
                )
            )

    for i in range(tiles):
        total[i * tile : (i + 1) * tile, :] = jnp.dot(
            ht[i * tile : (i + 1) * tile, :], joined[...], preferred_element_type=F32
        )
        for k in range(len(marks)):
            write(i, k, lambda copy: copy.start())
    for i in range(tiles):
        for k in range(len(marks)):
            write(i, k, lambda copy: copy.wait())


def call(kernel, name, outs, specs, mib, flops, scratch=(), alias=None):
    many = isinstance(outs, list)
    moved = sum(math.prod(x.shape) * 4 for x in (outs if many else [outs]))
    return pl.pallas_call(
        kernel,
        out_shape=outs,
        in_specs=specs,
        out_specs=[VM] * len(outs) if many else (ANY if "_product" in name else VM),
        scratch_shapes=list(scratch),
        input_output_aliases=alias or {},
        compiler_params=pltpu.CompilerParams(vmem_limit_bytes=mib << 20),
        cost_estimate=pl.CostEstimate(flops=flops, bytes_accessed=moved, transcendentals=0),
    )


def work(hidden, cotangent, routes, combine, block_pair, lengths, log_ratio):
    dp, groups, line = (lax.axis_size(name) for name in ("dp", "expert", "mp"))
    m = lax.axis_index("mp").astype(jnp.int32)
    tokens, top = routes.shape
    most = 3 * tokens // 4
    full = cotangent.shape[1]
    inner = hidden.shape[2]
    pair_of_cores = dp == 2
    halves = 2 if pair_of_cores else 1
    part = inner // halves
    early = full // 4 if pair_of_cores and full % 512 == 0 else 0
    width = full - early
    rows = groups * most
    pad = 8 * (-(-groups // 8))
    operands = (routes.T, combine.T, block_pair, lengths, log_ratio, cotangent)

    packed = call(
        functools.partial(pack_scaled, groups, most, early),
        "pack_scaled",
        [
            jax.ShapeDtypeStruct((pad, 128), F32),
            jax.ShapeDtypeStruct((pad, tokens), F32),
            jax.ShapeDtypeStruct((pad, tokens), F32),
            jax.ShapeDtypeStruct((top, tokens), jnp.int32),
            jax.ShapeDtypeStruct((tokens, max(early, 128)), BF16),
        ]
        + [jax.ShapeDtypeStruct((most, width), BF16)] * groups,
        [HBM] * 6,
        60,
        2 * groups * most * tokens * width,
        [pltpu.VMEM(x.shape, x.dtype) for x in operands[1:]] + [pltpu.SemaphoreType.DMA((6,))],
    )(*operands)
    load, key, shares, routes_held, raw = packed[:5]
    scaled = packed[5:]

    packed_h = [
        call(
            functools.partial(pack_hidden, groups, most, h, halves),
            f"pack_hidden{h}",
            [jax.ShapeDtypeStruct((most, part), BF16)] * groups,
            [VM, VM, VM],
            24,
            2 * rows * tokens * top * part,
        )(routes_held, key, hidden)
        for h in range(halves)
    ]

    arrived = [scaled[0]] + [
        lax.ppermute(scaled[j], "expert", pairs_of(groups, j)) for j in range(1, groups)
    ]
    blocks = []
    for h in range(halves):
        for j in range(groups):
            block = packed_h[h][j]
            if h:
                block = lax.ppermute(
                    block,
                    ("dp", "expert"),
                    [(a * groups + b, (a ^ h) * groups + c) for a in range(dp) for b, c in pairs_of(groups, j)],
                )
            elif j:
                block = lax.ppermute(block, "expert", pairs_of(groups, j))
            blocks.append(block)

    if not early:
        expert_load = lax.psum(load, ("dp", "expert"))[:groups, 0]

    def joined(name, kernel, *parts):
        count = rows if kernel is not join else sum(x.shape[0] for x in parts)
        return call(
            kernel, name, jax.ShapeDtypeStruct((count, parts[0].shape[1]), BF16), [VM] * len(parts), 8, 0
        )(*parts)

    up = [(i, i + 1) for i in range(line - 1)]
    down = [(i + 1, i) for i in range(line - 1)]
    start = joined("join", join, *arrived)
    below, above = [start], [start]
    for hop in range(1, line):
        below.append(lax.ppermute(below[-1], "mp", up[hop - 1 :]))
        above.append(lax.ppermute(above[-1], "mp", down[: line - hop]))

    shards = [(start, "below", 0)]
    for hop in range(1, line):
        if 2 * hop < line:
            shards.append((below[hop], "below", hop))
            shards.append((above[hop], "above", hop))
        else:
            either = functools.partial(join_either, hop)
            shards.append((joined(f"join{hop}", either, below[hop], above[hop]), "either", hop))

    if not pair_of_cores:
        hidden_rows = jnp.concatenate(blocks, axis=0)
        partial = jnp.zeros((inner, full * line), F32)
        for shard, which, hop in shards:
            piece = lax.dot_general(
                hidden_rows, shard, (((0,), (0,)), ((), ())), preferred_element_type=F32
            )
            low, high = m >= hop, m + hop < line
            valid = {"below": low, "above": high, "either": low | high}[which]
            at = jnp.where(low if which != "above" else False, m - hop, m + hop)
            at = jnp.clip(at, 0, line - 1) * full
            old = lax.dynamic_slice(partial, (0, at), piece.shape)
            partial = lax.dynamic_update_slice(partial, jnp.where(valid, piece, old), (0, at))
        owned = lax.psum_scatter(partial, "dp", scatter_dimension=0, tiled=True)
        return owned[None], expert_load

    step = 256 if (2 * rows) % 256 == 0 else most
    ht = call(
        functools.partial(turn, step),
        "turn",
        jax.ShapeDtypeStruct((part, 2 * rows), BF16),
        [VM] * len(blocks),
        20,
        2 * rows * part * 512,
        [pltpu.VMEM((2 * rows, part), BF16)],
    )(*blocks)
    tile = part // 2 if part % 16 == 0 else part
    out_shape = jax.ShapeDtypeStruct((part, full * line), F32)

    def swap(mine):
        return lax.ppermute(mine, "dp", [(0, 1), (1, 0)])

    def multiply(name, sources, steps, out):
        columns = sources[0].shape[1] * max(len(steps), 1)
        writes = len(steps) or line
        extra = [] if out is None else [out]
        return call(
            functools.partial(product, tile, line, steps),
            name,
            out_shape,
            [VM] * (1 + len(sources)) + [ANY] * len(extra),
            24,
            4 * part * rows * columns,
            [
                pltpu.VMEM((2 * rows, columns), BF16),
                pltpu.VMEM((part, columns), F32),
                pltpu.SemaphoreType.DMA((part // tile * writes,)),
            ],
            {} if out is None else {1 + len(sources): 0},
        )(ht, *sources, *extra)

    have = []
    for mine, which, hop in shards:
        have.append((mine, swap(mine), which, hop))
    out = None
    early_shards = have[:-1]
    first = early_shards[:1] + early_shards[-1:] if len(early_shards) > 1 else early_shards
    for i, group in enumerate((first, early_shards[1:-1])):
        for k in range(0, len(group), 2):
            some = group[k : k + 2]
            sources = [x for mine, theirs, _, _ in some for x in (mine, theirs)]
            steps = tuple((which, hop) for _, _, which, hop in some)
            out = multiply(f"pair_product{i}", sources, steps, out)
    if early:
        spread = [raw] + [
            lax.ppermute(raw, "mp", [(a, (a + k) % line) for a in range(line)])
            for k in range(1, line)
        ]
        sent = call(
            functools.partial(pack_early, most, line),
            "pack_early",
            [jax.ShapeDtypeStruct((most + 2 * pad, early * line), BF16)] * groups,
            [VM] * (3 + line),
            12,
            2 * rows * tokens * early * line,
        )(key, shares, load, *spread)
        kept = [sent[0]] + [
            lax.ppermute(sent[j], "expert", pairs_of(groups, j)) for j in range(1, groups)
        ]
        own = call(
            functools.partial(join_early, most),
            "join_early",
            jax.ShapeDtypeStruct((rows + 2 * pad, early * line), BF16),
            [VM] * groups,
            8,
            0,
        )(*kept)
        theirs = swap(own)
        out = multiply("early_product", [own, theirs], (), out)
        expert_load = call(
            functools.partial(tally, rows),
            "tally",
            jax.ShapeDtypeStruct((pad, 128), F32),
            [VM] * 2,
            8,
            0,
        )(own, theirs)[:groups, 0]
    mine, theirs, which, hop = have[-1]
    half = call(
        functools.partial(half_product, tile),
        "half",
        jax.ShapeDtypeStruct((part, width), F32),
        [VM, VM],
        16,
        2 * part * rows * width,
    )(ht, mine)
    out = call(
        functools.partial(last_product, tile, line, which, hop),
        "last_product",
        out_shape,
        [VM, VM, VM, ANY],
        20,
        2 * part * rows * width,
        [pltpu.VMEM((part, width), F32), pltpu.SemaphoreType.DMA((part // tile,))],
        {3: 0},
    )(ht, half, theirs, out)
    return out[None], expert_load


def solution(mesh):
    in_specs = (
        P(("dp", "expert"), None, "mp"),
        P(("dp", "expert"), "mp"),
        P(("dp", "expert"), None),
        P(("dp", "expert"), None),
        P(("dp", "expert"), None),
        P(("dp", "expert"), None),
        P(("dp", "expert"), None),
    )
    out_specs = (P("expert", ("mp", "dp"), None), P())
    step = jax.shard_map(work, mesh=mesh, in_specs=in_specs, out_specs=out_specs, check_vma=False)
    if tuple(mesh.shape[name] for name in ("dp", "expert", "mp")) != (2, 4, 4):
        return step
    return step
```

profile of v0, /device:TPU:0, one launch (start us, length us, event | category | flops | bytes accessed | tf_op | source)
XLA Modules:
  0.0 145.5 jit_solution(5382716034022464441)
XLA Ops:
  0.6 2.8 %shard_map.86 = (f32[8,128]{1,0:T(8,128)}, f32[8,384]{1,0:T(8,128)}, f32[8,384]{1,0:T(8,128)}, s32[2,384]{1,0:T(2,128)}, bf16[384,128]{1,0:T(8,128)(2,1)}, /*ind...) custom-call(s32[2,384]{1,0:T(2,128)} %bitcast.4, ...), custom_call_target="tpu_custom_call" | custom-call | flops 339738624 | bytes 1997824 | tf_op jit(solution)/shard_map/pallas_call | solution.py:294
  3.4 3.0 %collective-permute-start.7 = (bf16[288,384]{1,0:T(8,128)(2,1)}, bf16[288,384]{1,0:T(8,128)(2,1)S(1)}, u32[]{:S(2)}, u32[]{:S(2)}) collective-permute-start(bf16[288,384]{1,0:T(8,128)(2,1)} %get-tuple-element.34), channel_id=1, source_target_pairs={{0,4},{4,0},{8,12},{12,8},{1,5},{5,1},{9,13},{13,9},{2,6},{6,2},{1... | collective-permute-start | bytes 663560 | tf_op jit(solution)/shard_map/ppermute | solution.py:326
  6.4 1.5 %collective-permute-start.8 = (bf16[288,384]{1,0:T(8,128)(2,1)}, bf16[288,384]{1,0:T(8,128)(2,1)S(1)}, u32[]{:S(2)}, u32[]{:S(2)}) collective-permute-start(bf16[288,384]{1,0:T(8,128)(2,1)} %get-tuple-element.35), channel_id=1, source_target_pairs={{0,8},{4,12},{8,0},{12,4},{1,9},{5,13},{9,1},{13,5},{2,10},{6,14},... | collective-permute-start | bytes 663560 | tf_op jit(solution)/shard_map/ppermute | solution.py:326
  8.0 4.9 %collective-permute-done.7.refs_1_ = bf16[288,384]{1,0:T(8,128)(2,1)S(1)} collective-permute-done((bf16[288,384]{1,0:T(8,128)(2,1)}, bf16[288,384]{1,0:T(8,128)(2,1)S(1)}, u32[]{:S(2)}, u32[]{:S(2)}) %collective-permute-start.7) | collective-permute-done | bytes 221216 | tf_op jit(solution)/shard_map/ppermute | solution.py:326
  12.9 5.3 %collective-permute-done.8.refs_2_ = bf16[288,384]{1,0:T(8,128)(2,1)S(1)} collective-permute-done((bf16[288,384]{1,0:T(8,128)(2,1)}, bf16[288,384]{1,0:T(8,128)(2,1)S(1)}, u32[]{:S(2)}, u32[]{:S(2)}) %collective-permute-start.8) | collective-permute-done | bytes 221216 | tf_op jit(solution)/shard_map/ppermute | solution.py:326
  19.3 3.5 %collective-permute-start.10 = (bf16[1152,384]{1,0:T(8,128)(2,1)S(1)}, bf16[1152,384]{1,0:T(8,128)(2,1)S(1)}, u32[]{:S(2)}, u32[]{:S(2)}) collective-permute-start(bf16[1152,384]{1,0:T(8,128)(2,1)S(1)} %shard_map.90.refs_0_), channel_id=1, source_target_pairs={{0,1},{1,2},{2,3},{4,5},{5,6},{6,7},{8,9},{9,10},{10,11},{12,13},{... | collective-permute-start | bytes 2654216 | tf_op jit(solution)/shard_map/ppermute | solution.py:356
  24.1 2.7 %collective-permute-start.17 = (bf16[384,128]{1,0:T(8,128)(2,1)}, bf16[384,128]{1,0:T(8,128)(2,1)S(1)}, u32[]{:S(2)}, u32[]{:S(2)}) collective-permute-start(bf16[384,128]{1,0:T(8,128)(2,1)} %get-tuple-element.39.refs_0_), channel_id=1, source_target_pairs={{0,1},{1,2},{2,3},{3,0},{4,5},{5,6},{6,7},{7,4},{8,9},{9,10},{10,1... | collective-permute-start | bytes 294920 | tf_op jit(solution)/shard_map/ppermute | solution.py:433
  26.8 2.6 %collective-permute-start.18 = (bf16[384,128]{1,0:T(8,128)(2,1)}, bf16[384,128]{1,0:T(8,128)(2,1)S(1)}, u32[]{:S(2)}, u32[]{:S(2)}) collective-permute-start(bf16[384,128]{1,0:T(8,128)(2,1)} %get-tuple-element.39.refs_0_), channel_id=1, source_target_pairs={{0,2},{1,3},{2,0},{3,1},{4,6},{5,7},{6,4},{7,5},{8,10},{9,11},{10,... | collective-permute-start | bytes 294920 | tf_op jit(solution)/shard_map/ppermute | solution.py:433
  30.7 20.3 %collective-permute-done.17.refs_1_ = bf16[384,128]{1,0:T(8,128)(2,1)S(1)} collective-permute-done((bf16[384,128]{1,0:T(8,128)(2,1)}, bf16[384,128]{1,0:T(8,128)(2,1)S(1)}, u32[]{:S(2)}, u32[]{:S(2)}) %collective-permute-start.17) | collective-permute-done | bytes 98336 | tf_op jit(solution)/shard_map/ppermute | solution.py:433
  51.0 2.1 %collective-permute-done.18.refs_2_ = bf16[384,128]{1,0:T(8,128)(2,1)S(1)} collective-permute-done((bf16[384,128]{1,0:T(8,128)(2,1)}, bf16[384,128]{1,0:T(8,128)(2,1)S(1)}, u32[]{:S(2)}, u32[]{:S(2)}) %collective-permute-start.18) | collective-permute-done | bytes 98336 | tf_op jit(solution)/shard_map/ppermute | solution.py:433
  60.4 1.8 %copy-done.1 = bf16[384,2,1792]{2,1,0:T(2,128)(2,1)S(1)} copy-done((bf16[384,2,1792]{2,1,0:T(2,128)(2,1)S(1)}, bf16[384,2,1792]{2,1,0:T(2,128)(2,1)}, u32[]{:S(2)}) %copy-start.1) | copy-done | bytes 2752536
  63.6 2.1 %shard_map.88 = (bf16[288,896]{1,0:T(8,128)(2,1)S(1)}, bf16[288,896]{1,0:T(8,128)(2,1)S(1)}, bf16[288,896]{1,0:T(8,128)(2,1)S(1)}, bf16[288,896]{1,0:T(8,128)(2,1)S(1)}) custom-call(s32[2,384]{1,0:T(2,128)S(1)} %copy-done.7, f32[8,384]{1,0:T(8,128)S(1)} %copy-done.4, bf16[384,2,1792]{2,1,0:T(2,128)(2,1)S(1)} %copy-done.1), custom_call_target="tpu_custom_call" | custom-call | flops 1585446912 | bytes 4128768 | tf_op jit(solution)/shard_map/pallas_call | solution.py:314
  65.8 2.8 %collective-permute-done.21.refs_2_ = bf16[304,512]{1,0:T(8,128)(2,1)S(1)} collective-permute-done((bf16[304,512]{1,0:T(8,128)(2,1)S(1)}, bf16[304,512]{1,0:T(8,128)(2,1)S(1)}, u32[]{:S(2)}, u32[]{:S(2)}) %collective-permute-start.21) | collective-permute-done | bytes 311328 | tf_op jit(solution)/shard_map/ppermute | solution.py:445
  70.7 2.1 %shard_map.87 = (bf16[288,896]{1,0:T(8,128)(2,1)S(1)}, bf16[288,896]{1,0:T(8,128)(2,1)S(1)}, bf16[288,896]{1,0:T(8,128)(2,1)S(1)}, bf16[288,896]{1,0:T(8,128)(2,1)S(1)}) custom-call(s32[2,384]{1,0:T(2,128)S(1)} %copy-done.7, f32[8,384]{1,0:T(8,128)S(1)} %copy-done.4, bf16[384,2,1792]{2,1,0:T(2,128)(2,1)S(1)} %copy-done.1), custom_call_target="tpu_custom_call" | custom-call | flops 1585446912 | bytes 4128768 | tf_op jit(solution)/shard_map/pallas_call | solution.py:314
  72.9 1.8 %collective-permute-start.6 = (bf16[288,896]{1,0:T(8,128)(2,1)S(1)}, bf16[288,896]{1,0:T(8,128)(2,1)S(1)}, u32[]{:S(2)}, u32[]{:S(2)}) collective-permute-start(bf16[288,896]{1,0:T(8,128)(2,1)S(1)} %get-tuple-element.32), channel_id=1, source_target_pairs={{0,28},{4,24},{8,20},{12,16},{16,12},{20,8},{24,4},{28,0},{1,29},{... | collective-permute-start | bytes 1548296 | tf_op jit(solution)/shard_map/ppermute | solution.py:333
  74.7 8.0 %collective-permute-done.4.refs_5_ = bf16[288,896]{1,0:T(8,128)(2,1)S(1)} collective-permute-done((bf16[288,896]{1,0:T(8,128)(2,1)S(1)}, bf16[288,896]{1,0:T(8,128)(2,1)S(1)}, u32[]{:S(2)}, u32[]{:S(2)}) %collective-permute-start.4) | collective-permute-done | bytes 516128 | tf_op jit(solution)/shard_map/ppermute | solution.py:333
  83.3 10.2 %collective-permute-done.5.refs_6_ = bf16[288,896]{1,0:T(8,128)(2,1)S(1)} collective-permute-done((bf16[288,896]{1,0:T(8,128)(2,1)S(1)}, bf16[288,896]{1,0:T(8,128)(2,1)S(1)}, u32[]{:S(2)}, u32[]{:S(2)}) %collective-permute-start.5) | collective-permute-done | bytes 516128 | tf_op jit(solution)/shard_map/ppermute | solution.py:333
  95.9 7.2 %collective-permute-done.refs_1_ = bf16[288,896]{1,0:T(8,128)(2,1)S(1)} collective-permute-done((bf16[288,896]{1,0:T(8,128)(2,1)S(1)}, bf16[288,896]{1,0:T(8,128)(2,1)S(1)}, u32[]{:S(2)}, u32[]{:S(2)}) %collective-permute-start) | collective-permute-done | bytes 516128 | tf_op jit(solution)/shard_map/ppermute | solution.py:339
  105.8 14.3 %collective-permute-done.1.refs_2_ = bf16[288,896]{1,0:T(8,128)(2,1)S(1)} collective-permute-done((bf16[288,896]{1,0:T(8,128)(2,1)S(1)}, bf16[288,896]{1,0:T(8,128)(2,1)S(1)}, u32[]{:S(2)}, u32[]{:S(2)}) %collective-permute-start.1) | collective-permute-done | bytes 516128 | tf_op jit(solution)/shard_map/ppermute | solution.py:339
  122.3 6.1 %collective-permute-done.15.refs_1_ = bf16[1152,384]{1,0:T(8,128)(2,1)S(1)} collective-permute-done((bf16[1152,384]{1,0:T(8,128)(2,1)S(1)}, bf16[1152,384]{1,0:T(8,128)(2,1)S(1)}, u32[]{:S(2)}, u32[]{:S(2)}) %collective-permute-start.15) | collective-permute-done | bytes 884768 | tf_op jit(solution)/shard_map/ppermute | solution.py:357
  130.7 4.6 %shard_map.96.refs_4_ = f32[896,2048]{1,0:T(8,128)} custom-call(bf16[896,2304]{1,0:T(8,128)(2,1)S(1)} %shard_map.89.ht, bf16[1152,384]{1,0:T(8,128)(2,1)S(1)} %shard_map.90.refs_0_, bf16[1152,384]{1,0:T(8,128)(2,1)S(1)} %collective-permute-done.26.refs_1_, bf16[1152,384]{1,0:T(8,128)(2,1)S(1)} %shard_map.95.refs_2_, ...), custom_call_target="tpu_custom_call" | custom-call | flops 3170893824 | bytes 7340032 | tf_op jit(solution)/shard_map/pallas_call | solution.py:404
  135.4 4.4 %shard_map.97.refs_2_ = f32[896,2048]{1,0:T(8,128)} custom-call(bf16[896,2304]{1,0:T(8,128)(2,1)S(1)} %shard_map.89.ht, bf16[1152,384]{1,0:T(8,128)(2,1)S(1)} %collective-permute-done.10.refs_0_, bf16[1152,384]{1,0:T(8,128)(2,1)S(1)} %collective-permute-done.24.refs_1_, ...), custom_call_target="tpu_custom_call", output_to_operand_aliasing={{}: (5, {})} | custom-call | flops 3170893824 | bytes 7340032 | tf_op jit(solution)/shard_map/pallas_call | solution.py:404
  139.8 3.3 %shard_map.98._ = f32[896,2048]{1,0:T(8,128)} custom-call(bf16[896,2304]{1,0:T(8,128)(2,1)S(1)} %shard_map.89.ht, bf16[1168,512]{1,0:T(8,128)(2,1)S(1)} %shard_map.94.refs_0_.mine, bf16[1168,512]{1,0:T(8,128)(2,1)S(1)} %collective-permute-done.23.refs_1_.theirs, f32[896,2048]{1,0:T(8,128)} %shard_map.97.refs_2_), custom_call_target="tpu_custom_call", output_to_operand_aliasing={{}: (3, {})} | custom-call | flops 2113929216 | bytes 7340032 | tf_op jit(solution)/shard_map/pallas_call | solution.py:404
  143.1 2.2 %shard_map.99 = f32[896,2048]{1,0:T(8,128)} custom-call(bf16[896,2304]{1,0:T(8,128)(2,1)S(1)} %shard_map.89.ht, f32[896,384]{1,0:T(8,128)S(1)} %shard_map.92.first, bf16[1152,384]{1,0:T(8,128)(2,1)S(1)} %collective-permute-done.16.theirs, f32[896,2048]{1,0:T(8,128)} %shard_map.98._), custom_call_target="tpu_custom_call", output_to_operand_aliasing={{}: (3, {})} | custom-call | flops 792723456 | bytes 7340032 | tf_op jit(solution)/shard_map/pallas_call | solution.py:474
  (64 shorter events, 24.6 us)
Async XLA Ops:
  6.4 11.8 %collective-permute-start.8 = (bf16[288,384]{1,0:T(8,128)(2,1)}, bf16[288,384]{1,0:T(8,128)(2,1)S(1)}, u32[]{:S(2)}, u32[]{:S(2)}) collective-permute-start(bf16[288,384]{1,0:T(8,128)(2,1)} %get-tuple-element.35), channel_id=1, source_target_pairs={{0,8},{4,12},{8,0},{12,4},{1,9},{5,13},{9,1},{13,5},{2,10},{6,14},... | collective-permute-start | bytes 663560 | tf_op jit(solution)/shard_map/ppermute | solution.py:326
  7.9 10.3 %collective-permute-start.9 = (bf16[288,384]{1,0:T(8,128)(2,1)}, bf16[288,384]{1,0:T(8,128)(2,1)S(1)}, u32[]{:S(2)}, u32[]{:S(2)}) collective-permute-start(bf16[288,384]{1,0:T(8,128)(2,1)} %get-tuple-element.36), channel_id=1, source_target_pairs={{0,12},{4,8},{8,4},{12,0},{1,13},{5,9},{9,5},{13,1},{2,14},{6,10},... | collective-permute-start | bytes 663560 | tf_op jit(solution)/shard_map/ppermute | solution.py:326
  19.3 49.3 %collective-permute-start.10 = (bf16[1152,384]{1,0:T(8,128)(2,1)S(1)}, bf16[1152,384]{1,0:T(8,128)(2,1)S(1)}, u32[]{:S(2)}, u32[]{:S(2)}) collective-permute-start(bf16[1152,384]{1,0:T(8,128)(2,1)S(1)} %shard_map.90.refs_0_), channel_id=1, source_target_pairs={{0,1},{1,2},{2,3},{4,5},{5,6},{6,7},{8,9},{9,10},{10,11},{12,13},{... | collective-permute-start | bytes 2654216 | tf_op jit(solution)/shard_map/ppermute | solution.py:356
  22.8 46.6 %collective-permute-start.13 = (bf16[1152,384]{1,0:T(8,128)(2,1)S(1)}, bf16[1152,384]{1,0:T(8,128)(2,1)S(1)}, u32[]{:S(2)}, u32[]{:S(2)}) collective-permute-start(bf16[1152,384]{1,0:T(8,128)(2,1)S(1)} %shard_map.90.refs_0_), channel_id=1, source_target_pairs={{1,0},{2,1},{3,2},{5,4},{6,5},{7,6},{9,8},{10,9},{11,10},{13,12},{... | collective-permute-start | bytes 2654216 | tf_op jit(solution)/shard_map/ppermute | solution.py:357
  24.1 26.9 %collective-permute-start.17 = (bf16[384,128]{1,0:T(8,128)(2,1)}, bf16[384,128]{1,0:T(8,128)(2,1)S(1)}, u32[]{:S(2)}, u32[]{:S(2)}) collective-permute-start(bf16[384,128]{1,0:T(8,128)(2,1)} %get-tuple-element.39.refs_0_), channel_id=1, source_target_pairs={{0,1},{1,2},{2,3},{3,0},{4,5},{5,6},{6,7},{7,4},{8,9},{9,10},{10,1... | collective-permute-start | bytes 294920 | tf_op jit(solution)/shard_map/ppermute | solution.py:433
  26.8 26.3 %collective-permute-start.18 = (bf16[384,128]{1,0:T(8,128)(2,1)}, bf16[384,128]{1,0:T(8,128)(2,1)S(1)}, u32[]{:S(2)}, u32[]{:S(2)}) collective-permute-start(bf16[384,128]{1,0:T(8,128)(2,1)} %get-tuple-element.39.refs_0_), channel_id=1, source_target_pairs={{0,2},{1,3},{2,0},{3,1},{4,6},{5,7},{6,4},{7,5},{8,10},{9,11},{10,... | collective-permute-start | bytes 294920 | tf_op jit(solution)/shard_map/ppermute | solution.py:433
  29.4 23.7 %collective-permute-start.19 = (bf16[384,128]{1,0:T(8,128)(2,1)}, bf16[384,128]{1,0:T(8,128)(2,1)S(1)}, u32[]{:S(2)}, u32[]{:S(2)}) collective-permute-start(bf16[384,128]{1,0:T(8,128)(2,1)} %get-tuple-element.39.refs_0_), channel_id=1, source_target_pairs={{0,3},{1,0},{2,1},{3,2},{4,7},{5,4},{6,5},{7,6},{8,11},{9,8},{10,9... | collective-permute-start | bytes 294920 | tf_op jit(solution)/shard_map/ppermute | solution.py:433
  58.9 10.4 %collective-permute-start.22 = (bf16[304,512]{1,0:T(8,128)(2,1)S(1)}, bf16[304,512]{1,0:T(8,128)(2,1)S(1)}, u32[]{:S(2)}, u32[]{:S(2)}) collective-permute-start(bf16[304,512]{1,0:T(8,128)(2,1)S(1)} %get-tuple-element.43), channel_id=1, source_target_pairs={{0,12},{4,8},{8,4},{12,0},{1,13},{5,9},{9,5},{13,1},{2,14},{6,10},... | collective-permute-start | bytes 933896 | tf_op jit(solution)/shard_map/ppermute | solution.py:445
  68.6 14.0 %collective-permute-start.4 = (bf16[288,896]{1,0:T(8,128)(2,1)S(1)}, bf16[288,896]{1,0:T(8,128)(2,1)S(1)}, u32[]{:S(2)}, u32[]{:S(2)}) collective-permute-start(bf16[288,896]{1,0:T(8,128)(2,1)S(1)} %get-tuple-element.30), channel_id=1, source_target_pairs={{0,20},{4,16},{8,28},{12,24},{16,4},{20,0},{24,12},{28,8},{1,21},{... | collective-permute-start | bytes 1548296 | tf_op jit(solution)/shard_map/ppermute | solution.py:333
  68.6 26.0 %collective-permute-start.11 = (bf16[1152,384]{1,0:T(8,128)(2,1)S(1)}, bf16[1152,384]{1,0:T(8,128)(2,1)S(1)}, u32[]{:S(2)}, u32[]{:S(2)}) collective-permute-start(bf16[1152,384]{1,0:T(8,128)(2,1)S(1)} %collective-permute-done.10.refs_0_), channel_id=1, source_target_pairs={{1,2},{2,3},{5,6},{6,7},{9,10},{10,11},{13,14},{14,15},{17,18},{18... | collective-permute-start | bytes 2654216 | tf_op jit(solution)/shard_map/ppermute | solution.py:356
  69.4 24.2 %collective-permute-start.5 = (bf16[288,896]{1,0:T(8,128)(2,1)S(1)}, bf16[288,896]{1,0:T(8,128)(2,1)S(1)}, u32[]{:S(2)}, u32[]{:S(2)}) collective-permute-start(bf16[288,896]{1,0:T(8,128)(2,1)S(1)} %get-tuple-element.31), channel_id=1, source_target_pairs={{0,24},{4,28},{8,16},{12,20},{16,8},{20,12},{24,0},{28,4},{1,25},{... | collective-permute-start | bytes 1548296 | tf_op jit(solution)/shard_map/ppermute | solution.py:333
  69.4 35.0 %collective-permute-start.14 = (bf16[1152,384]{1,0:T(8,128)(2,1)S(1)}, bf16[1152,384]{1,0:T(8,128)(2,1)S(1)}, u32[]{:S(2)}, u32[]{:S(2)}) collective-permute-start(bf16[1152,384]{1,0:T(8,128)(2,1)S(1)} %collective-permute-done.13.refs_2_), channel_id=1, source_target_pairs={{1,0},{2,1},{5,4},{6,5},{9,8},{10,9},{13,12},{14,13},{17,16},{18,1... | collective-permute-start | bytes 2654216 | tf_op jit(solution)/shard_map/ppermute | solution.py:357
  72.9 22.5 %collective-permute-start.6 = (bf16[288,896]{1,0:T(8,128)(2,1)S(1)}, bf16[288,896]{1,0:T(8,128)(2,1)S(1)}, u32[]{:S(2)}, u32[]{:S(2)}) collective-permute-start(bf16[288,896]{1,0:T(8,128)(2,1)S(1)} %get-tuple-element.32), channel_id=1, source_target_pairs={{0,28},{4,24},{8,20},{12,16},{16,12},{20,8},{24,4},{28,0},{1,29},{... | collective-permute-start | bytes 1548296 | tf_op jit(solution)/shard_map/ppermute | solution.py:333
  82.7 20.4 %collective-permute-start = (bf16[288,896]{1,0:T(8,128)(2,1)S(1)}, bf16[288,896]{1,0:T(8,128)(2,1)S(1)}, u32[]{:S(2)}, u32[]{:S(2)}) collective-permute-start(bf16[288,896]{1,0:T(8,128)(2,1)S(1)} %get-tuple-element.26), channel_id=1, source_target_pairs={{0,4},{4,0},{8,12},{12,8},{1,5},{5,1},{9,13},{13,9},{2,6},{6,2},{1... | collective-permute-start | bytes 1548296 | tf_op jit(solution)/shard_map/ppermute | solution.py:339
  93.5 27.2 %collective-permute-start.23 = (bf16[1168,512]{1,0:T(8,128)(2,1)S(1)}, bf16[1168,512]{1,0:T(8,128)(2,1)S(1)}, u32[]{:S(2)}, u32[]{:S(2)}) collective-permute-start(bf16[1168,512]{1,0:T(8,128)(2,1)S(1)} %shard_map.94.refs_0_.mine), channel_id=1, source_target_pairs={{0,16},{16,0},{1,17},{17,1},{2,18},{18,2},{3,19},{19,3},{4,20},{20... | collective-permute-start | bytes 3588104 | tf_op jit(solution)/shard_map/ppermute | solution.py:398
  94.6 26.1 %collective-permute-start.12 = (bf16[1152,384]{1,0:T(8,128)(2,1)S(1)}, bf16[1152,384]{1,0:T(8,128)(2,1)S(1)}, u32[]{:S(2)}, u32[]{:S(2)}) collective-permute-start(bf16[1152,384]{1,0:T(8,128)(2,1)S(1)} %collective-permute-done.11.refs_0_), channel_id=1, source_target_pairs={{2,3},{6,7},{10,11},{14,15},{18,19},{22,23},{26,27},{30,31}} | collective-permute-start | bytes 2654216 | tf_op jit(solution)/shard_map/ppermute | solution.py:356
  95.4 24.8 %collective-permute-start.1 = (bf16[288,896]{1,0:T(8,128)(2,1)S(1)}, bf16[288,896]{1,0:T(8,128)(2,1)S(1)}, u32[]{:S(2)}, u32[]{:S(2)}) collective-permute-start(bf16[288,896]{1,0:T(8,128)(2,1)S(1)} %get-tuple-element.27), channel_id=1, source_target_pairs={{0,8},{4,12},{8,0},{12,4},{1,9},{5,13},{9,1},{13,5},{2,10},{6,14},... | collective-permute-start | bytes 1548296 | tf_op jit(solution)/shard_map/ppermute | solution.py:339
  103.1 17.0 %collective-permute-start.2 = (bf16[288,896]{1,0:T(8,128)(2,1)S(1)}, bf16[288,896]{1,0:T(8,128)(2,1)S(1)}, u32[]{:S(2)}, u32[]{:S(2)}) collective-permute-start(bf16[288,896]{1,0:T(8,128)(2,1)S(1)} %get-tuple-element.28), channel_id=1, source_target_pairs={{0,12},{4,8},{8,4},{12,0},{1,13},{5,9},{9,5},{13,1},{2,14},{6,10},... | collective-permute-start | bytes 1548296 | tf_op jit(solution)/shard_map/ppermute | solution.py:339
  104.4 24.0 %collective-permute-start.15 = (bf16[1152,384]{1,0:T(8,128)(2,1)S(1)}, bf16[1152,384]{1,0:T(8,128)(2,1)S(1)}, u32[]{:S(2)}, u32[]{:S(2)}) collective-permute-start(bf16[1152,384]{1,0:T(8,128)(2,1)S(1)} %collective-permute-done.14.refs_1_), channel_id=1, source_target_pairs={{1,0},{5,4},{9,8},{13,12},{17,16},{21,20},{25,24},{29,28}} | collective-permute-start | bytes 2654216 | tf_op jit(solution)/shard_map/ppermute | solution.py:357
  120.2 10.6 %collective-permute-start.26 = (bf16[1152,384]{1,0:T(8,128)(2,1)S(1)}, bf16[1152,384]{1,0:T(8,128)(2,1)S(1)}, u32[]{:S(2)}, u32[]{:S(2)}) collective-permute-start(bf16[1152,384]{1,0:T(8,128)(2,1)S(1)} %shard_map.90.refs_0_), channel_id=1, source_target_pairs={{0,16},{16,0},{1,17},{17,1},{2,18},{18,2},{3,19},{19,3},{4,20},{20... | collective-permute-start | bytes 2654216 | tf_op jit(solution)/shard_map/ppermute | solution.py:398
  120.2 10.6 %collective-permute-start.27 = (bf16[1152,384]{1,0:T(8,128)(2,1)S(1)}, bf16[1152,384]{1,0:T(8,128)(2,1)S(1)}, u32[]{:S(2)}, u32[]{:S(2)}) collective-permute-start(bf16[1152,384]{1,0:T(8,128)(2,1)S(1)} %shard_map.95.refs_2_), channel_id=1, source_target_pairs={{0,16},{16,0},{1,17},{17,1},{2,18},{18,2},{3,19},{19,3},{4,20},{20... | collective-permute-start | bytes 2654216 | tf_op jit(solution)/shard_map/ppermute | solution.py:398
  120.7 14.7 %collective-permute-start.24 = (bf16[1152,384]{1,0:T(8,128)(2,1)S(1)}, bf16[1152,384]{1,0:T(8,128)(2,1)S(1)}, u32[]{:S(2)}, u32[]{:S(2)}) collective-permute-start(bf16[1152,384]{1,0:T(8,128)(2,1)S(1)} %collective-permute-done.10.refs_0_), channel_id=1, source_target_pairs={{0,16},{16,0},{1,17},{17,1},{2,18},{18,2},{3,19},{19,3},{4,20},{20... | collective-permute-start | bytes 2654216 | tf_op jit(solution)/shard_map/ppermute | solution.py:398
  120.7 14.7 %collective-permute-start.25 = (bf16[1152,384]{1,0:T(8,128)(2,1)S(1)}, bf16[1152,384]{1,0:T(8,128)(2,1)S(1)}, u32[]{:S(2)}, u32[]{:S(2)}) collective-permute-start(bf16[1152,384]{1,0:T(8,128)(2,1)S(1)} %collective-permute-done.13.refs_2_), channel_id=1, source_target_pairs={{0,16},{16,0},{1,17},{17,1},{2,18},{18,2},{3,19},{19,3},{4,20},{20... | collective-permute-start | bytes 2654216 | tf_op jit(solution)/shard_map/ppermute | solution.py:398
  128.7 14.4 %collective-permute-start.16 = (bf16[1152,384]{1,0:T(8,128)(2,1)S(1)}, bf16[1152,384]{1,0:T(8,128)(2,1)S(1)}, u32[]{:S(2)}, u32[]{:S(2)}) collective-permute-start(bf16[1152,384]{1,0:T(8,128)(2,1)S(1)} %shard_map.91.mine), channel_id=1, source_target_pairs={{0,16},{16,0},{1,17},{17,1},{2,18},{18,2},{3,19},{19,3},{4,20},{20... | collective-permute-start | bytes 2654216 | tf_op jit(solution)/shard_map/ppermute | solution.py:398
  (12 other events, 42.8 us)
where the time goes:
time: 146 us; the launch traced here: 145 us
  waiting for transfers between devices  81.3 us (56%)
  starting transfers between devices  30.1 us (21%)
  Pallas kernels  25.3 us (17%)
  local copies, waits for them, and re-layouts  7.71 us (5%)
    ppermute x3, waiting for transfers between devices, work(): lax.ppermute(raw, 'mp', [(a, (a + k) % line) for a in range(line)])  22.4 us
    ppermute x3, waiting for transfers between devices, work(): block = lax.ppermute(block, 'expert', pairs_of(groups, j))  21.6 us
    ppermute x4, waiting for transfers between devices, work(): lax.ppermute(block, ('dp', 'expert'), [(a * groups + b, (a ^ h) * groups...  18.1 us
    pallas_call x3, Pallas kernels, multiply(): call(functools.partial(product, tile, line, steps), name, out_shape, [VM]...  12.3 us
    ppermute x3, waiting for transfers between devices, work(): lax.ppermute(scaled[j], 'expert', pairs_of(groups, j))  10.3 us
    unnamed x16, local copies, waits for them, and re-layouts  7.08 us
    ppermute x3, starting transfers between devices, work(): lax.ppermute(raw, 'mp', [(a, (a + k) % line) for a in range(line)])  6.58 us
    ppermute x3, waiting for transfers between devices, work(): above.append(lax.ppermute(above[-1], 'mp', down[:line - hop]))  6.12 us
  transfers between devices with their start and end apart: 28, of which 10 were waited for; matrix products, arithmetic and copies ran while one was open for 0% of the time, Pallas kernels for 14%

commit v1 on v0

v1 whole, which is shorter than its diff:
```python
import functools
import math
import jax
import jax.numpy as jnp
from jax import lax
from jax.experimental import pallas as pl
from jax.experimental.pallas import tpu as pltpu
from jax.sharding import PartitionSpec as P


BETA = 0.1
F32 = jnp.float32
BF16 = jnp.bfloat16
VM = pl.BlockSpec(memory_space=pltpu.VMEM)
ANY = pl.BlockSpec(memory_space=pl.ANY)
HBM = pl.BlockSpec(memory_space=pltpu.HBM)


def iota(shape, dim):
    return lax.broadcasted_iota(jnp.int32, shape, dim)


def other(place, hop, size):
    return place ^ hop if size & (size - 1) == 0 else lax.rem(place + hop, size)


def pairs_of(size, hop):
    return [(i, i ^ hop if size & (size - 1) == 0 else (i + hop) % size) for i in range(size)]


def pack_scaled(groups, most, early, *refs):
    table, raw = refs[6:8]
    scaled = refs[8 : 8 + groups]
    routes, combine, pair, lengths, ratio, cot, sem = refs[8 + groups :]
    copies = [
        pltpu.make_async_copy(source, held, sem.at[i])
        for i, (source, held) in enumerate(zip(refs[:6], (routes, combine, pair, lengths, ratio, cot)))
    ]
    for copy in copies:
        copy.start()
    for copy in copies[:-1]:
        copy.wait()
    blocks = pair.shape[1]
    rows = routes.shape[1]
    length = rows // blocks
    pair_row = jnp.broadcast_to(pair[...], (blocks, blocks))
    ratio_row = jnp.broadcast_to(ratio[...], (blocks, blocks))
    length_row = jnp.broadcast_to(lengths[...], (blocks, blocks))
    eye = iota((blocks, blocks), 0) == iota((blocks, blocks), 1)
    pair_col = jnp.sum(jnp.where(eye, pair_row, 0), axis=1, keepdims=True)
    length_col = jnp.sum(jnp.where(eye, length_row, 0), axis=1, keepdims=True)
    chosen = jnp.sum(jnp.where(pair_row == (pair_col & -2), ratio_row, 0.0), axis=1, keepdims=True)
    refused = jnp.sum(jnp.where(pair_row == (pair_col | 1), ratio_row, 0.0), axis=1, keepdims=True)
    coef = BETA * jax.nn.sigmoid(-BETA * (chosen - refused))
    block_weight = jnp.where((pair_col & 1) == 0, -coef, coef)
    owner = iota((blocks, rows), 1) // length == iota((blocks, rows), 0)
    weight = jnp.sum(jnp.where(owner, block_weight, 0.0), axis=0, keepdims=True)
    valid = jnp.sum(jnp.where(owner, length_col, 0), axis=0, keepdims=True)
    live = iota((1, rows), 1) % length < valid
    weight = jnp.where(live, weight, 0.0)
    first, second = routes[0:1, :], routes[1:2, :]
    weight0, weight1 = combine[0:1, :] * weight, combine[1:2, :] * weight
    pad = -(-groups // 8) * 8
    label = iota((pad, rows), 0)
    counted = ((first == label) | (second == label)) & live
    counts = jnp.sum(jnp.where(counted, 1.0, 0.0), axis=1, keepdims=True)
    named = other(jnp.full((pad, rows), lax.axis_index("expert"), jnp.int32), label, groups)
    hit0, hit1 = first == named, second == named
    hit = hit0 | hit1
    before = jnp.where(iota((rows, rows), 0) < iota((rows, rows), 1), 1.0, 0.0).astype(BF16)
    rank = jnp.dot(jnp.where(hit, 1.0, 0.0).astype(BF16), before, preferred_element_type=F32)
    key = jnp.where(hit, rank, -1.0)
    by_group = jnp.where(hit0, weight0, jnp.where(hit1, weight1, 0.0))
    routed = jnp.where(label == 0, first, second).astype(F32)
    table[...] = jnp.concatenate(
        [key, by_group, routed, jnp.broadcast_to(counts, (pad, rows))], axis=0
    )
    copies[-1].wait()
    raw[...] = cot[:, : raw.shape[1]]
    place_scaled(most, key, by_group, cot[:, early:], scaled)


def place_scaled(most, key, by_group, source, outs):
    slot = iota((most, key.shape[1]), 0).astype(F32)
    for j, out in enumerate(outs):
        at = slot == key[j : j + 1, :]
        row_weight = jnp.sum(jnp.where(at, by_group[j : j + 1, :], 0.0), axis=1, keepdims=True)
        taken = jnp.dot(jnp.where(at, 1.0, 0.0).astype(BF16), source, preferred_element_type=F32)
        out[:most, :] = (row_weight * taken).astype(BF16)


def pack_early(most, line, table, *refs):
    source, outs = jnp.concatenate([x[...] for x in refs[:line]], axis=1), refs[line:]
    pad = table.shape[0] // 4
    place_scaled(most, table[:pad], table[pad : 2 * pad], source, outs)
    counts = split_counts(table[3 * pad :, :1], source.shape[1])
    for out in outs:
        out[most:, :] = counts


def split_counts(counts, columns):
    high = jnp.floor(counts * (1.0 / 128.0))
    both = jnp.concatenate([high, counts - 128.0 * high], axis=0)
    return jnp.broadcast_to(both, (both.shape[0], columns)).astype(BF16)


def read_counts(rows):
    rows = rows.astype(F32)
    half = rows.shape[0] // 2
    return 128.0 * rows[:half] + rows[half:]


def join_early(most, *refs):
    blocks, out = refs[:-1], refs[-1]
    counts = sum(read_counts(block[most:, :128]) for block in blocks)
    for i, block in enumerate(blocks):
        out[i * most : (i + 1) * most, :] = block[:most, :]
    out[len(blocks) * most :, :] = split_counts(counts[:, :1], out.shape[1])


def tally(rows, mine, theirs, out):
    out[...] = read_counts(mine[rows:, :128]) + read_counts(theirs[rows:, :128])


def pack_hidden(groups, most, hop, halves, table, hidden, *outs):
    rows, top, inner = hidden.shape
    width = inner // halves
    flat = rows * top
    part = other(lax.axis_index("dp"), hop, halves) if halves > 1 else 0
    columns = pl.ds(pl.multiple_of(part * width, 128), width)
    pad = table.shape[0] // 4
    key, routes = table[:pad], table[2 * pad : 3 * pad]
    spread = jnp.where(iota((rows, flat), 0) == iota((rows, flat), 1) // top, 1.0, 0.0).astype(BF16)
    high = jnp.floor(key * (1.0 / 16.0))
    named = [jnp.broadcast_to(routes[k : k + 1], (pad, rows)) for k in range(top)]
    stacked = jnp.concatenate([high, key - 16.0 * high] + named, axis=0).astype(BF16)
    wide = jnp.dot(stacked, spread, preferred_element_type=F32)
    key = 16.0 * wide[:pad] + wide[pad : 2 * pad]
    choice = iota((pad, flat), 1) % top
    route = wide[2 * pad : 3 * pad]
    for k in range(1, top):
        route = jnp.where(choice == k, wide[(2 + k) * pad : (3 + k) * pad], route)
    me = jnp.full((pad, flat), lax.axis_index("expert"), jnp.int32)
    label = other(me, iota((pad, flat), 0), groups).astype(F32)
    key = jnp.where(route == label, key, -1.0)
    slot = iota((most, flat), 0).astype(F32)
    source = hidden[:, :, columns].reshape(flat, width)
    for j in range(groups):
        at = jnp.where(slot == key[j : j + 1, :], 1.0, 0.0).astype(BF16)
        outs[j][...] = jnp.dot(at, source, preferred_element_type=F32).astype(BF16)


def turn(step, *refs):
    blocks, out, joined = refs[:-2], refs[-2], refs[-1]
    most = blocks[0].shape[0]
    for i, block in enumerate(blocks):
        joined[i * most : (i + 1) * most, :] = block[...]
    for i in range(0, joined.shape[0], step):
        out[:, i : i + step] = joined[i : i + step, :].T


def stack_into(out, parts):
    at = 0
    for part in parts:
        out[at : at + part.shape[0], :] = part[...]
        at += part.shape[0]


def join(*refs):
    stack_into(refs[-1], refs[:-1])


def pick(inner, outer, out):
    m = lax.axis_index("mp")
    at_end = (m == 0) | (m == lax.axis_size("mp") - 1)

    @pl.when(at_end)
    def _():
        out[...] = outer[...]

    @pl.when(jnp.logical_not(at_end))
    def _():
        out[...] = inner[...]


def shard_at(step):
    m = lax.axis_index("mp")
    low = m < 2
    return (m, m ^ 1, jnp.where(low, 2, 1), jnp.where(low, 3, 0))[step]


def half_product(tile, ht, mine, out):
    for i in range(0, ht.shape[0], tile):
        out[i : i + tile, :] = jnp.dot(
            ht[i : i + tile, :], mine[: ht.shape[1], :], preferred_element_type=F32
        )


def product(tile, line, steps, ht, *refs):
    count = len(steps)
    halves, theirs = refs[:count], refs[count : 2 * count]
    out, joined, total, sem = refs[-4:]
    rows = ht.shape[1]
    shard = out.shape[1] // line
    m = lax.axis_index("mp")
    marks, at = [], 0
    for step, x in zip(steps, theirs):
        width = x.shape[1]
        joined[:, at : at + width] = x[:rows, :]
        if step < 0:
            size = width // line
            marks += [(lax.rem(m + line - k, line) * shard, at + k * size, size) for k in range(line)]
        else:
            marks.append((shard_at(step) * shard + shard - width, at, width))
        at += width
    copies = []
    for i in range(0, ht.shape[0], tile):
        second = jnp.dot(ht[i : i + tile, :], joined[...], preferred_element_type=F32)
        at = 0
        for half in halves:
            columns = slice(at, at + half.shape[1])
            total[i : i + tile, columns] = half[i : i + tile, :] + second[:, columns]
            at += half.shape[1]
        for k, (column, at, size) in enumerate(marks):
            copy = pltpu.make_async_copy(
                total.at[pl.ds(i, tile), pl.ds(at, size)],
                out.at[pl.ds(i, tile), pl.ds(pl.multiple_of(column, 128), size)],
                sem.at[i // tile * len(marks) + k],
            )
            copy.start()
            copies.append(copy)
    for copy in copies:
        copy.wait()


def call(kernel, name, outs, specs, mib, flops, scratch=(), alias=None):
    many = isinstance(outs, list)
    moved = sum(math.prod(x.shape) * 4 for x in (outs if many else [outs]))
    return pl.pallas_call(
        kernel,
        out_shape=outs,
        in_specs=specs,
        out_specs=[VM] * len(outs) if many else (ANY if "_product" in name else VM),
        scratch_shapes=list(scratch),
        input_output_aliases=alias or {},
        compiler_params=pltpu.CompilerParams(vmem_limit_bytes=mib << 20),
        cost_estimate=pl.CostEstimate(flops=flops, bytes_accessed=moved, transcendentals=0),
    )


def work(hidden, cotangent, routes, combine, block_pair, lengths, log_ratio):
    dp, groups, line = (lax.axis_size(name) for name in ("dp", "expert", "mp"))
    tokens, top = routes.shape
    most = 3 * tokens // 4
    full = cotangent.shape[1]
    inner = hidden.shape[2]
    fast = dp == 2 and line == 4 and full % 512 == 0 and inner % 256 == 0
    halves = 2 if fast else 1
    part = inner // halves
    early = full // 4 if fast else 0
    width = full - early
    rows = groups * most
    pad = 8 * (-(-groups // 8))
    operands = (routes.T, combine.T, block_pair, lengths, log_ratio, cotangent)

    packed = call(
        functools.partial(pack_scaled, groups, most, early),
        "pack_scaled",
        [
            jax.ShapeDtypeStruct((4 * pad, tokens), F32),
            jax.ShapeDtypeStruct((tokens, max(early, 128)), BF16),
        ]
        + [jax.ShapeDtypeStruct((most, width), BF16)] * groups,
        [HBM] * 6,
        60,
        2 * groups * most * tokens * width,
        [pltpu.VMEM(x.shape, x.dtype) for x in operands] + [pltpu.SemaphoreType.DMA((6,))],
    )(*operands)
    table, raw = packed[:2]
    scaled = packed[2:]

    packed_h = [
        call(
            functools.partial(pack_hidden, groups, most, h, halves),
            f"pack_hidden{h}",
            [jax.ShapeDtypeStruct((most, part), BF16)] * groups,
            [VM, VM],
            24,
            2 * rows * tokens * top * part,
        )(table, hidden)
        for h in range(halves)
    ]

    arrived = [scaled[0]] + [
        lax.ppermute(scaled[j], "expert", pairs_of(groups, j)) for j in range(1, groups)
    ]
    blocks = []
    for h in range(halves):
        for j in range(groups):
            block = packed_h[h][j]
            if h:
                block = lax.ppermute(
                    block,
                    ("dp", "expert"),
                    [(a * groups + b, (a ^ h) * groups + c) for a in range(dp) for b, c in pairs_of(groups, j)],
                )
            elif j:
                block = lax.ppermute(block, "expert", pairs_of(groups, j))
            blocks.append(block)

    start = call(
        join, "join", jax.ShapeDtypeStruct((rows, width), BF16), [VM] * groups, 8, 0
    )(*arrived)
    if not fast:
        expert_load = lax.psum(table[3 * pad : 3 * pad + groups, 0], ("dp", "expert"))
        gathered = lax.all_gather(start, "mp", axis=1, tiled=True)
        partial = lax.dot_general(
            jnp.concatenate(blocks, axis=0),
            gathered,
            (((0,), (0,)), ((), ())),
            preferred_element_type=F32,
        )
        owned = lax.psum_scatter(partial, "dp", scatter_dimension=0, tiled=True)
        return owned[None], expert_load

    pairs, middle, outward = [(0, 1), (1, 0), (2, 3), (3, 2)], [(1, 2), (2, 1)], [(1, 0), (2, 3)]
    p1, q1 = lax.ppermute(start, "mp", pairs), lax.ppermute(start, "mp", middle)
    q2, p2 = lax.ppermute(p1, "mp", middle), lax.ppermute(q1, "mp", outward)
    p3 = lax.ppermute(q2, "mp", outward)

    def picked(name, inner_rows, outer_rows):
        return call(pick, name, jax.ShapeDtypeStruct((rows, width), BF16), [VM] * 2, 8, 0)(
            inner_rows, outer_rows
        )

    shards = [start, p1, picked("pick2", q1, p2), picked("pick3", q2, p3)]

    step = 128 if rows % 128 == 0 else most
    turned = [
        call(
            functools.partial(turn, step),
            f"turn{h}",
            jax.ShapeDtypeStruct((part, rows), BF16),
            [VM] * groups,
            12,
            rows * part * 512,
            [pltpu.VMEM((rows, part), BF16)],
        )(*blocks[h * groups : (h + 1) * groups])
        for h in range(halves)
    ]
    tile = part // 4 if part % 32 == 0 else part
    out_shape = jax.ShapeDtypeStruct((part, full * line), F32)

    def swap(mine):
        return lax.ppermute(mine, "dp", [(0, 1), (1, 0)])

    def half(name, mine):
        return call(
            functools.partial(half_product, tile),
            name,
            jax.ShapeDtypeStruct((part, mine.shape[1]), F32),
            [VM, VM],
            12,
            2 * part * rows * mine.shape[1],
        )(turned[0], mine)

    def finish(name, halves, theirs, steps, out):
        columns = sum(x.shape[1] for x in theirs)
        writes = len(steps) + (line - 1 if -1 in steps else 0)
        extra = [] if out is None else [out]
        return call(
            functools.partial(product, tile, line, steps),
            name,
            out_shape,
            [VM] * (1 + 2 * len(theirs)) + [ANY] * len(extra),
            20,
            2 * part * rows * columns,
            [
                pltpu.VMEM((rows, columns), BF16),
                pltpu.VMEM((part, columns), F32),
                pltpu.SemaphoreType.DMA((part // tile * writes,)),
            ],
            {} if out is None else {1 + 2 * len(theirs): 0},
        )(turned[1], *halves, *theirs, *extra)

    own = [half(f"half{i}", x) for i, x in enumerate(shards)]
    theirs = [swap(x) for x in shards]
    out = finish("pair_product", own[:2], theirs[:2], (0, 1), None)
    out = finish("next_product", own[2:3], theirs[2:3], (2,), out)
    spread = [raw] + [
        lax.ppermute(raw, "mp", [(a, (a + k) % line) for a in range(line)])
        for k in range(1, line)
    ]
    sent = call(
        functools.partial(pack_early, most, line),
        "pack_early",
        [jax.ShapeDtypeStruct((most + 2 * pad, early * line), BF16)] * groups,
        [VM] * (1 + line),
        12,
        2 * rows * tokens * early * line,
    )(table, *spread)
    kept = [sent[0]] + [
        lax.ppermute(sent[j], "expert", pairs_of(groups, j)) for j in range(1, groups)
    ]
    mine = call(
        functools.partial(join_early, most),
        "join_early",
        jax.ShapeDtypeStruct((rows + 2 * pad, early * line), BF16),
        [VM] * groups,
        8,
        0,
    )(*kept)
    other_core = swap(mine)
    out = finish(
        "last_product",
        [half("half_early", mine), own[3]],
        [other_core, theirs[3]],
        (-1, 3),
        out,
    )
    expert_load = call(
        functools.partial(tally, rows),
        "tally",
        jax.ShapeDtypeStruct((pad, 128), F32),
        [VM] * 2,
        8,
        0,
    )(mine, other_core)[:groups, 0]
    return out[None], expert_load


def solution(mesh):
    in_specs = (
        P(("dp", "expert"), None, "mp"),
        P(("dp", "expert"), "mp"),
        P(("dp", "expert"), None),
        P(("dp", "expert"), None),
        P(("dp", "expert"), None),
        P(("dp", "expert"), None),
        P(("dp", "expert"), None),
    )
    out_specs = (P("expert", ("mp", "dp"), None), P())
    step = jax.shard_map(work, mesh=mesh, in_specs=in_specs, out_specs=out_specs, check_vma=False)
    if tuple(mesh.shape[name] for name in ("dp", "expert", "mp")) != (2, 4, 4):
        return step
    return step
```

time: 146 us -> 141 us (0.966)
  local copies, waits for them, and re-layouts: 7.71 us -> 4.05 us
  starting transfers between devices: 30.1 us -> 27.5 us
  waiting for transfers between devices: 81.3 us -> 83.7 us
    ppermute x6 -> x5, waiting for transfers between devices: 6.13 us -> 20.7 us  [the longest x1 18.7 us: work(): p3 = lax.ppermute(q2, 'mp', outward)]
    ppermute x3, waiting for transfers between devices: 21.6 us -> 7.28 us  [work(): block = lax.ppermute(block, 'expert', pairs_of(groups, j))]
    ppermute x3, waiting for transfers between devices: 2.78 us -> 14.1 us  [work(): lax.ppermute(sent[j], 'expert', pairs_of(groups, j))]
    ppermute x4, waiting for transfers between devices: 18.1 us -> 11.7 us  [work(): lax.ppermute(block, ('dp', 'expert'), [(a * groups + b, (a ^ h) * groups...]
    unnamed x16 -> x10, local copies, waits for them, and re-layouts: 7.08 us -> 3.42 us
    ppermute x6 -> x5, starting transfers between devices: 8.81 us -> 5.62 us  [the longest x2 2 us: work(): q2, p2 = (lax.ppermute(p1, 'mp', middle), lax.ppermute(q1, 'mp', outward))]
    ppermute x3, waiting for transfers between devices: 22.4 us -> 19.5 us  [work(): lax.ppermute(raw, 'mp', [(a, (a + k) % line) for a in range(line)])]
    ppermute x3, starting transfers between devices: 2.41 us -> 5.19 us  [work(): block = lax.ppermute(block, 'expert', pairs_of(groups, j))]
  transfers between devices with their start and end apart: 28 -> 26, of which waited for: 10 -> 11; matrix products, arithmetic and copies ran while one was open for 0% -> 0% of each run, Pallas kernels for 14% -> 13%
where the time goes in v1:
time: 141 us
  waiting for transfers between devices  83.7 us (59%)
  starting transfers between devices  27.5 us (20%)
  Pallas kernels  24.5 us (17%)
  local copies, waits for them, and re-layouts  4.05 us (3%)
    ppermute x3, waiting for transfers between devices, work(): lax.ppermute(raw, 'mp', [(a, (a + k) % line) for a in range(line)])  19.5 us
    ppermute x1, waiting for transfers between devices, work(): p3 = lax.ppermute(q2, 'mp', outward)  18.7 us
    ppermute x3, waiting for transfers between devices, work(): lax.ppermute(sent[j], 'expert', pairs_of(groups, j))  14.1 us
    ppermute x4, waiting for transfers between devices, work(): lax.ppermute(block, ('dp', 'expert'), [(a * groups + b, (a ^ h) * groups...  11.7 us
    ppermute x3, waiting for transfers between devices, work(): lax.ppermute(scaled[j], 'expert', pairs_of(groups, j))  10.3 us
    pallas_call x3, Pallas kernels, finish(): call(functools.partial(product, tile, line, steps), name, out_shape, [VM]...  8.55 us
    ppermute x3, waiting for transfers between devices, work(): block = lax.ppermute(block, 'expert', pairs_of(groups, j))  7.28 us
    pallas_call x5, Pallas kernels, half(): call(functools.partial(half_product, tile), name, jax.ShapeDtypeStruct((p...  6.55 us
  transfers between devices with their start and end apart: 26, of which 11 were waited for; matrix products, arithmetic and copies ran while one was open for 0% of the time, Pallas kernels for 13%

profile of v1, /device:TPU:0, one launch (start us, length us, event | category | flops | bytes accessed | tf_op | source)
XLA Modules:
  0.0 140.7 jit_solution(1994248495221525017)
XLA Ops:
  0.6 2.6 %shard_map.86 = (f32[32,384]{1,0:T(8,128)}, bf16[384,128]{1,0:T(8,128)(2,1)}, bf16[288,384]{1,0:T(8,128)(2,1)}, bf16[288,384]{1,0:T(8,128)(2,1)}, bf16[288,384]{1,0:T(8,128)(2,1)}, /*index=5*/bf16[288,384]{1,0:T(8,128)(2,1)}) custom-call(s32[2,384]{1,0:T(2,128)} %bitcast.4, f32[2,384]{1,0:T(2,128)} %bitcast.5, s32[1,12]{1,0:T(1,128)} %refs_2_.1, ...), custom_call_target="tpu_custom_call" | custom-call | flops 339738624 | bytes 2015232 | tf_op jit(solution)/shard_map/pallas_call | solution.py:266
  3.2 3.0 %collective-permute-start.13 = (bf16[288,384]{1,0:T(8,128)(2,1)}, bf16[288,384]{1,0:T(8,128)(2,1)S(1)}, u32[]{:S(2)}, u32[]{:S(2)}) collective-permute-start(bf16[288,384]{1,0:T(8,128)(2,1)} %get-tuple-element.35), channel_id=1, source_target_pairs={{0,4},{4,0},{8,12},{12,8},{1,5},{5,1},{9,13},{13,9},{2,6},{6,2},{1... | collective-permute-start | bytes 663560 | tf_op jit(solution)/shard_map/ppermute | solution.py:295
  6.3 1.5 %collective-permute-start.14 = (bf16[288,384]{1,0:T(8,128)(2,1)}, bf16[288,384]{1,0:T(8,128)(2,1)S(1)}, u32[]{:S(2)}, u32[]{:S(2)}) collective-permute-start(bf16[288,384]{1,0:T(8,128)(2,1)} %get-tuple-element.36), channel_id=1, source_target_pairs={{0,8},{4,12},{8,0},{12,4},{1,9},{5,13},{9,1},{13,5},{2,10},{6,14},... | collective-permute-start | bytes 663560 | tf_op jit(solution)/shard_map/ppermute | solution.py:295
  7.8 5.0 %collective-permute-done.13.refs_1_ = bf16[288,384]{1,0:T(8,128)(2,1)S(1)} collective-permute-done((bf16[288,384]{1,0:T(8,128)(2,1)}, bf16[288,384]{1,0:T(8,128)(2,1)S(1)}, u32[]{:S(2)}, u32[]{:S(2)}) %collective-permute-start.13) | collective-permute-done | bytes 221216 | tf_op jit(solution)/shard_map/ppermute | solution.py:295
  12.8 5.3 %collective-permute-done.14.refs_2_ = bf16[288,384]{1,0:T(8,128)(2,1)S(1)} collective-permute-done((bf16[288,384]{1,0:T(8,128)(2,1)}, bf16[288,384]{1,0:T(8,128)(2,1)S(1)}, u32[]{:S(2)}, u32[]{:S(2)}) %collective-permute-start.14) | collective-permute-done | bytes 221216 | tf_op jit(solution)/shard_map/ppermute | solution.py:295
  19.1 1.6 %collective-permute-start.16 = (bf16[1152,384]{1,0:T(8,128)(2,1)S(1)}, bf16[1152,384]{1,0:T(8,128)(2,1)S(1)}, u32[]{:S(2)}, u32[]{:S(2)}) collective-permute-start(bf16[1152,384]{1,0:T(8,128)(2,1)S(1)} %shard_map.94.mine), channel_id=1, source_target_pairs={{0,1},{1,0},{2,3},{3,2},{4,5},{5,4},{6,7},{7,6},{8,9},{9,8},{10,11... | collective-permute-start | bytes 2654216 | tf_op jit(solution)/shard_map/ppermute | solution.py:327
  21.2 2.6 %collective-permute-start.8 = (bf16[384,128]{1,0:T(8,128)(2,1)}, bf16[384,128]{1,0:T(8,128)(2,1)S(1)}, u32[]{:S(2)}, u32[]{:S(2)}) collective-permute-start(bf16[384,128]{1,0:T(8,128)(2,1)} %get-tuple-element.29.refs_0_), channel_id=1, source_target_pairs={{0,2},{1,3},{2,0},{3,1},{4,6},{5,7},{6,4},{7,5},{8,10},{9,11},{10,... | collective-permute-start | bytes 294920 | tf_op jit(solution)/shard_map/ppermute | solution.py:391
  23.8 2.5 %collective-permute-start.9 = (bf16[384,128]{1,0:T(8,128)(2,1)}, bf16[384,128]{1,0:T(8,128)(2,1)S(1)}, u32[]{:S(2)}, u32[]{:S(2)}) collective-permute-start(bf16[384,128]{1,0:T(8,128)(2,1)} %get-tuple-element.29.refs_0_), channel_id=1, source_target_pairs={{0,3},{1,0},{2,1},{3,2},{4,7},{5,4},{6,5},{7,6},{8,11},{9,8},{10,9... | collective-permute-start | bytes 294920 | tf_op jit(solution)/shard_map/ppermute | solution.py:391
  26.3 19.5 %collective-permute-done.7.refs_1_ = bf16[384,128]{1,0:T(8,128)(2,1)S(1)} collective-permute-done((bf16[384,128]{1,0:T(8,128)(2,1)}, bf16[384,128]{1,0:T(8,128)(2,1)S(1)}, u32[]{:S(2)}, u32[]{:S(2)}) %collective-permute-start.7) | collective-permute-done | bytes 98336 | tf_op jit(solution)/shard_map/ppermute | solution.py:391
  48.3 1.5 %collective-permute-start.10 = (bf16[304,512]{1,0:T(8,128)(2,1)S(1)}, bf16[304,512]{1,0:T(8,128)(2,1)S(1)}, u32[]{:S(2)}, u32[]{:S(2)}) collective-permute-start(bf16[304,512]{1,0:T(8,128)(2,1)S(1)} %get-tuple-element.31), channel_id=1, source_target_pairs={{0,4},{4,0},{8,12},{12,8},{1,5},{5,1},{9,13},{13,9},{2,6},{6,2},{1... | collective-permute-start | bytes 933896 | tf_op jit(solution)/shard_map/ppermute | solution.py:403
  52.7 2.1 %shard_map.89 = (bf16[288,896]{1,0:T(8,128)(2,1)S(1)}, bf16[288,896]{1,0:T(8,128)(2,1)S(1)}, bf16[288,896]{1,0:T(8,128)(2,1)S(1)}, bf16[288,896]{1,0:T(8,128)(2,1)S(1)}) custom-call(f32[32,384]{1,0:T(8,128)S(1)} %copy-done.4, bf16[384,2,1792]{2,1,0:T(2,128)(2,1)S(1)} %copy-done.1), custom_call_target="tpu_custom_call" | custom-call | flops 1585446912 | bytes 4128768 | tf_op jit(solution)/shard_map/pallas_call | solution.py:283
  56.6 1.3 collective-permute-start.12
  58.4 2.2 %collective-permute-start.5 = (bf16[288,896]{1,0:T(8,128)(2,1)S(1)}, bf16[288,896]{1,0:T(8,128)(2,1)S(1)}, u32[]{:S(2)}, u32[]{:S(2)}) collective-permute-start(bf16[288,896]{1,0:T(8,128)(2,1)S(1)} %get-tuple-element.27), channel_id=1, source_target_pairs={{0,8},{4,12},{8,0},{12,4},{1,9},{5,13},{9,1},{13,5},{2,10},{6,14},... | collective-permute-start | bytes 1548296 | tf_op jit(solution)/shard_map/ppermute | solution.py:308
  60.6 12.5 %collective-permute-done.12.refs_3_ = bf16[304,512]{1,0:T(8,128)(2,1)S(1)} collective-permute-done((bf16[304,512]{1,0:T(8,128)(2,1)S(1)}, bf16[304,512]{1,0:T(8,128)(2,1)S(1)}, u32[]{:S(2)}, u32[]{:S(2)}) %collective-permute-start.12) | collective-permute-done | bytes 311328 | tf_op jit(solution)/shard_map/ppermute | solution.py:403
  73.1 2.4 %collective-permute-start.6 = (bf16[288,896]{1,0:T(8,128)(2,1)S(1)}, bf16[288,896]{1,0:T(8,128)(2,1)S(1)}, u32[]{:S(2)}, u32[]{:S(2)}) collective-permute-start(bf16[288,896]{1,0:T(8,128)(2,1)S(1)} %get-tuple-element.28), channel_id=1, source_target_pairs={{0,12},{4,8},{8,4},{12,0},{1,13},{5,9},{9,5},{13,1},{2,14},{6,10},... | collective-permute-start | bytes 1548296 | tf_op jit(solution)/shard_map/ppermute | solution.py:308
  75.5 2.1 %shard_map.87 = (bf16[288,896]{1,0:T(8,128)(2,1)S(1)}, bf16[288,896]{1,0:T(8,128)(2,1)S(1)}, bf16[288,896]{1,0:T(8,128)(2,1)S(1)}, bf16[288,896]{1,0:T(8,128)(2,1)S(1)}) custom-call(f32[32,384]{1,0:T(8,128)S(1)} %copy-done.4, bf16[384,2,1792]{2,1,0:T(2,128)(2,1)S(1)} %copy-done.1), custom_call_target="tpu_custom_call" | custom-call | flops 1585446912 | bytes 4128768 | tf_op jit(solution)/shard_map/pallas_call | solution.py:283
  79.0 7.3 %collective-permute-done.5.refs_2_ = bf16[288,896]{1,0:T(8,128)(2,1)S(1)} collective-permute-done((bf16[288,896]{1,0:T(8,128)(2,1)S(1)}, bf16[288,896]{1,0:T(8,128)(2,1)S(1)}, u32[]{:S(2)}, u32[]{:S(2)}) %collective-permute-start.5) | collective-permute-done | bytes 516128 | tf_op jit(solution)/shard_map/ppermute | solution.py:308
  89.0 10.5 %collective-permute-done.1.refs_1_ = bf16[288,896]{1,0:T(8,128)(2,1)S(1)} collective-permute-done((bf16[288,896]{1,0:T(8,128)(2,1)S(1)}, bf16[288,896]{1,0:T(8,128)(2,1)S(1)}, u32[]{:S(2)}, u32[]{:S(2)}) %collective-permute-start.1) | collective-permute-done | bytes 516128 | tf_op jit(solution)/shard_map/ppermute | solution.py:302
  101.8 2.1 %collective-permute-done.22.outer = bf16[1152,384]{1,0:T(8,128)(2,1)S(1)} collective-permute-done((bf16[1152,384]{1,0:T(8,128)(2,1)S(1)}, bf16[1152,384]{1,0:T(8,128)(2,1)S(1)}, u32[]{:S(2)}, u32[]{:S(2)}) %collective-permute-start.22) | collective-permute-done | bytes 884768 | tf_op jit(solution)/shard_map/ppermute | solution.py:328
  104.0 18.7 %collective-permute-done.18.outer = bf16[1152,384]{1,0:T(8,128)(2,1)S(1)} collective-permute-done((bf16[1152,384]{1,0:T(8,128)(2,1)S(1)}, bf16[1152,384]{1,0:T(8,128)(2,1)S(1)}, u32[]{:S(2)}, u32[]{:S(2)}) %collective-permute-start.18) | collective-permute-done | bytes 884768 | tf_op jit(solution)/shard_map/ppermute | solution.py:329
  126.0 1.3 shard_map.93.refs_0_
  130.6 2.9 %shard_map.101.refs_2_ = f32[896,2048]{1,0:T(8,128)} custom-call(bf16[896,1152]{1,0:T(8,128)(2,1)S(1)} %shard_map.88.ht, f32[896,384]{1,0:T(8,128)S(1)} %shard_map.99.refs_0_, f32[896,384]{1,0:T(8,128)S(1)} %shard_map.100.refs_1_, bf16[1152,384]{1,0:T(8,128)(2,1)S(1)} %collective-permute-done.24.refs_2_, bf16[1152,384]{1,0:T(8,128)(2,1)S(1)} %collective-permute-done.25.refs_3_), custom_call_target="tpu_custom_call" | custom-call | flops 1585446912 | bytes 7340032 | tf_op jit(solution)/shard_map/pallas_call | solution.py:371
  134.9 2.1 %shard_map.102.refs_4_ = f32[896,2048]{1,0:T(8,128)} custom-call(bf16[896,1152]{1,0:T(8,128)(2,1)S(1)} %shard_map.88.ht, f32[896,384]{1,0:T(8,128)S(1)} %shard_map.98.refs_0_, bf16[1152,384]{1,0:T(8,128)(2,1)S(1)} %collective-permute-done.23.refs_1_, f32[896,2048]{1,0:T(8,128)} %shard_map.101.refs_2_), custom_call_target="tpu_custom_call", output_to_operand_aliasing={{}: (3, {})} | custom-call | flops 792723456 | bytes 7340032 | tf_op jit(solution)/shard_map/pallas_call | solution.py:371
  137.0 3.6 %shard_map.103 = f32[896,2048]{1,0:T(8,128)} custom-call(bf16[896,1152]{1,0:T(8,128)(2,1)S(1)} %shard_map.88.ht, f32[896,512]{1,0:T(8,128)S(1)} %shard_map.93.refs_0_, f32[896,384]{1,0:T(8,128)S(1)} %shard_map.96.refs_1_, bf16[1168,512]{1,0:T(8,128)(2,1)S(1)} %collective-permute-done.19.refs_2_.theirs, ...), custom_call_target="tpu_custom_call", output_to_operand_aliasing={{}: (5, {})} | custom-call | flops 1849688064 | bytes 7340032 | tf_op jit(solution)/shard_map/pallas_call | solution.py:371
  (58 shorter events, 23.4 us)
Async XLA Ops:
  3.2 9.5 %collective-permute-start.13 = (bf16[288,384]{1,0:T(8,128)(2,1)}, bf16[288,384]{1,0:T(8,128)(2,1)S(1)}, u32[]{:S(2)}, u32[]{:S(2)}) collective-permute-start(bf16[288,384]{1,0:T(8,128)(2,1)} %get-tuple-element.35), channel_id=1, source_target_pairs={{0,4},{4,0},{8,12},{12,8},{1,5},{5,1},{9,13},{13,9},{2,6},{6,2},{1... | collective-permute-start | bytes 663560 | tf_op jit(solution)/shard_map/ppermute | solution.py:295
  6.3 11.8 %collective-permute-start.14 = (bf16[288,384]{1,0:T(8,128)(2,1)}, bf16[288,384]{1,0:T(8,128)(2,1)S(1)}, u32[]{:S(2)}, u32[]{:S(2)}) collective-permute-start(bf16[288,384]{1,0:T(8,128)(2,1)} %get-tuple-element.36), channel_id=1, source_target_pairs={{0,8},{4,12},{8,0},{12,4},{1,9},{5,13},{9,1},{13,5},{2,10},{6,14},... | collective-permute-start | bytes 663560 | tf_op jit(solution)/shard_map/ppermute | solution.py:295
  7.8 10.3 %collective-permute-start.15 = (bf16[288,384]{1,0:T(8,128)(2,1)}, bf16[288,384]{1,0:T(8,128)(2,1)S(1)}, u32[]{:S(2)}, u32[]{:S(2)}) collective-permute-start(bf16[288,384]{1,0:T(8,128)(2,1)} %get-tuple-element.37), channel_id=1, source_target_pairs={{0,12},{4,8},{8,4},{12,0},{1,13},{5,9},{9,5},{13,1},{2,14},{6,10},... | collective-permute-start | bytes 663560 | tf_op jit(solution)/shard_map/ppermute | solution.py:295
  19.1 32.0 %collective-permute-start.16 = (bf16[1152,384]{1,0:T(8,128)(2,1)S(1)}, bf16[1152,384]{1,0:T(8,128)(2,1)S(1)}, u32[]{:S(2)}, u32[]{:S(2)}) collective-permute-start(bf16[1152,384]{1,0:T(8,128)(2,1)S(1)} %shard_map.94.mine), channel_id=1, source_target_pairs={{0,1},{1,0},{2,3},{3,2},{4,5},{5,4},{6,7},{7,6},{8,9},{9,8},{10,11... | collective-permute-start | bytes 2654216 | tf_op jit(solution)/shard_map/ppermute | solution.py:327
  20.8 25.1 %collective-permute-start.7 = (bf16[384,128]{1,0:T(8,128)(2,1)}, bf16[384,128]{1,0:T(8,128)(2,1)S(1)}, u32[]{:S(2)}, u32[]{:S(2)}) collective-permute-start(bf16[384,128]{1,0:T(8,128)(2,1)} %get-tuple-element.29.refs_0_), channel_id=1, source_target_pairs={{0,1},{1,2},{2,3},{3,0},{4,5},{5,6},{6,7},{7,4},{8,9},{9,10},{10,1... | collective-permute-start | bytes 294920 | tf_op jit(solution)/shard_map/ppermute | solution.py:391
  21.2 24.6 %collective-permute-start.8 = (bf16[384,128]{1,0:T(8,128)(2,1)}, bf16[384,128]{1,0:T(8,128)(2,1)S(1)}, u32[]{:S(2)}, u32[]{:S(2)}) collective-permute-start(bf16[384,128]{1,0:T(8,128)(2,1)} %get-tuple-element.29.refs_0_), channel_id=1, source_target_pairs={{0,2},{1,3},{2,0},{3,1},{4,6},{5,7},{6,4},{7,5},{8,10},{9,11},{10,... | collective-permute-start | bytes 294920 | tf_op jit(solution)/shard_map/ppermute | solution.py:391
  23.8 22.0 %collective-permute-start.9 = (bf16[384,128]{1,0:T(8,128)(2,1)}, bf16[384,128]{1,0:T(8,128)(2,1)S(1)}, u32[]{:S(2)}, u32[]{:S(2)}) collective-permute-start(bf16[384,128]{1,0:T(8,128)(2,1)} %get-tuple-element.29.refs_0_), channel_id=1, source_target_pairs={{0,3},{1,0},{2,1},{3,2},{4,7},{5,4},{6,5},{7,6},{8,11},{9,8},{10,9... | collective-permute-start | bytes 294920 | tf_op jit(solution)/shard_map/ppermute | solution.py:391
  49.8 27.9 %collective-permute-start.21 = (bf16[1152,384]{1,0:T(8,128)(2,1)S(1)}, bf16[1152,384]{1,0:T(8,128)(2,1)S(1)}, u32[]{:S(2)}, u32[]{:S(2)}) collective-permute-start(bf16[1152,384]{1,0:T(8,128)(2,1)S(1)} %shard_map.94.mine), channel_id=1, source_target_pairs={{1,2},{2,1},{5,6},{6,5},{9,10},{10,9},{13,14},{14,13},{17,18},{18,... | collective-permute-start | bytes 2654216 | tf_op jit(solution)/shard_map/ppermute | solution.py:327
  51.2 35.1 %collective-permute-start.17 = (bf16[1152,384]{1,0:T(8,128)(2,1)S(1)}, bf16[1152,384]{1,0:T(8,128)(2,1)S(1)}, u32[]{:S(2)}, u32[]{:S(2)}) collective-permute-start(bf16[1152,384]{1,0:T(8,128)(2,1)S(1)} %collective-permute-done.16.mine), channel_id=1, source_target_pairs={{1,2},{2,1},{5,6},{6,5},{9,10},{10,9},{13,14},{14,13},{17,18},{18,... | collective-permute-start | bytes 2654216 | tf_op jit(solution)/shard_map/ppermute | solution.py:328
  54.9 22.8 %collective-permute-start.4 = (bf16[288,896]{1,0:T(8,128)(2,1)S(1)}, bf16[288,896]{1,0:T(8,128)(2,1)S(1)}, u32[]{:S(2)}, u32[]{:S(2)}) collective-permute-start(bf16[288,896]{1,0:T(8,128)(2,1)S(1)} %get-tuple-element.26), channel_id=1, source_target_pairs={{0,4},{4,0},{8,12},{12,8},{1,5},{5,1},{9,13},{13,9},{2,6},{6,2},{1... | collective-permute-start | bytes 1548296 | tf_op jit(solution)/shard_map/ppermute | solution.py:308
  56.6 16.5 %collective-permute-start.12 = (bf16[304,512]{1,0:T(8,128)(2,1)S(1)}, bf16[304,512]{1,0:T(8,128)(2,1)S(1)}, u32[]{:S(2)}, u32[]{:S(2)}) collective-permute-start(bf16[304,512]{1,0:T(8,128)(2,1)S(1)} %get-tuple-element.33), channel_id=1, source_target_pairs={{0,12},{4,8},{8,4},{12,0},{1,13},{5,9},{9,5},{13,1},{2,14},{6,10},... | collective-permute-start | bytes 933896 | tf_op jit(solution)/shard_map/ppermute | solution.py:403
  58.4 27.9 %collective-permute-start.5 = (bf16[288,896]{1,0:T(8,128)(2,1)S(1)}, bf16[288,896]{1,0:T(8,128)(2,1)S(1)}, u32[]{:S(2)}, u32[]{:S(2)}) collective-permute-start(bf16[288,896]{1,0:T(8,128)(2,1)S(1)} %get-tuple-element.27), channel_id=1, source_target_pairs={{0,8},{4,12},{8,0},{12,4},{1,9},{5,13},{9,1},{13,5},{2,10},{6,14},... | collective-permute-start | bytes 1548296 | tf_op jit(solution)/shard_map/ppermute | solution.py:308
  73.1 14.5 %collective-permute-start.6 = (bf16[288,896]{1,0:T(8,128)(2,1)S(1)}, bf16[288,896]{1,0:T(8,128)(2,1)S(1)}, u32[]{:S(2)}, u32[]{:S(2)}) collective-permute-start(bf16[288,896]{1,0:T(8,128)(2,1)S(1)} %get-tuple-element.28), channel_id=1, source_target_pairs={{0,12},{4,8},{8,4},{12,0},{1,13},{5,9},{9,5},{13,1},{2,14},{6,10},... | collective-permute-start | bytes 1548296 | tf_op jit(solution)/shard_map/ppermute | solution.py:308
  77.6 10.1 %collective-permute-start = (bf16[288,896]{1,0:T(8,128)(2,1)S(1)}, bf16[288,896]{1,0:T(8,128)(2,1)S(1)}, u32[]{:S(2)}, u32[]{:S(2)}) collective-permute-start(bf16[288,896]{1,0:T(8,128)(2,1)S(1)} %get-tuple-element.21), channel_id=1, source_target_pairs={{0,16},{4,20},{8,24},{12,28},{16,0},{20,4},{24,8},{28,12},{1,17},{... | collective-permute-start | bytes 1548296 | tf_op jit(solution)/shard_map/ppermute | solution.py:302
  77.7 26.2 %collective-permute-start.22 = (bf16[1152,384]{1,0:T(8,128)(2,1)S(1)}, bf16[1152,384]{1,0:T(8,128)(2,1)S(1)}, u32[]{:S(2)}, u32[]{:S(2)}) collective-permute-start(bf16[1152,384]{1,0:T(8,128)(2,1)S(1)} %collective-permute-done.21.inner), channel_id=1, source_target_pairs={{1,0},{2,3},{5,4},{6,7},{9,8},{10,11},{13,12},{14,15},{17,16},{18,... | collective-permute-start | bytes 2654216 | tf_op jit(solution)/shard_map/ppermute | solution.py:328
  86.3 13.2 %collective-permute-start.1 = (bf16[288,896]{1,0:T(8,128)(2,1)S(1)}, bf16[288,896]{1,0:T(8,128)(2,1)S(1)}, u32[]{:S(2)}, u32[]{:S(2)}) collective-permute-start(bf16[288,896]{1,0:T(8,128)(2,1)S(1)} %get-tuple-element.22), channel_id=1, source_target_pairs={{0,20},{4,16},{8,28},{12,24},{16,4},{20,0},{24,12},{28,8},{1,21},{... | collective-permute-start | bytes 1548296 | tf_op jit(solution)/shard_map/ppermute | solution.py:302
  86.3 36.4 %collective-permute-start.18 = (bf16[1152,384]{1,0:T(8,128)(2,1)S(1)}, bf16[1152,384]{1,0:T(8,128)(2,1)S(1)}, u32[]{:S(2)}, u32[]{:S(2)}) collective-permute-start(bf16[1152,384]{1,0:T(8,128)(2,1)S(1)} %collective-permute-done.17.inner), channel_id=1, source_target_pairs={{1,0},{2,3},{5,4},{6,7},{9,8},{10,11},{13,12},{14,15},{17,16},{18,... | collective-permute-start | bytes 2654216 | tf_op jit(solution)/shard_map/ppermute | solution.py:329
  87.6 13.2 %collective-permute-start.2 = (bf16[288,896]{1,0:T(8,128)(2,1)S(1)}, bf16[288,896]{1,0:T(8,128)(2,1)S(1)}, u32[]{:S(2)}, u32[]{:S(2)}) collective-permute-start(bf16[288,896]{1,0:T(8,128)(2,1)S(1)} %get-tuple-element.23), channel_id=1, source_target_pairs={{0,24},{4,28},{8,16},{12,20},{16,8},{20,12},{24,0},{28,4},{1,25},{... | collective-permute-start | bytes 1548296 | tf_op jit(solution)/shard_map/ppermute | solution.py:302
  87.8 40.9 %collective-permute-start.19 = (bf16[1168,512]{1,0:T(8,128)(2,1)S(1)}, bf16[1168,512]{1,0:T(8,128)(2,1)S(1)}, u32[]{:S(2)}, u32[]{:S(2)}) collective-permute-start(bf16[1168,512]{1,0:T(8,128)(2,1)S(1)} %shard_map.92.mine), channel_id=1, source_target_pairs={{0,16},{16,0},{1,17},{17,1},{2,18},{18,2},{3,19},{19,3},{4,20},{20... | collective-permute-start | bytes 3588104 | tf_op jit(solution)/shard_map/ppermute | solution.py:355
  99.5 23.4 %collective-permute-start.3 = (bf16[288,896]{1,0:T(8,128)(2,1)S(1)}, bf16[288,896]{1,0:T(8,128)(2,1)S(1)}, u32[]{:S(2)}, u32[]{:S(2)}) collective-permute-start(bf16[288,896]{1,0:T(8,128)(2,1)S(1)} %get-tuple-element.24), channel_id=1, source_target_pairs={{0,28},{4,24},{8,20},{12,16},{16,12},{20,8},{24,4},{28,0},{1,29},{... | collective-permute-start | bytes 1548296 | tf_op jit(solution)/shard_map/ppermute | solution.py:302
  100.9 29.8 %collective-permute-start.24 = (bf16[1152,384]{1,0:T(8,128)(2,1)S(1)}, bf16[1152,384]{1,0:T(8,128)(2,1)S(1)}, u32[]{:S(2)}, u32[]{:S(2)}) collective-permute-start(bf16[1152,384]{1,0:T(8,128)(2,1)S(1)} %shard_map.94.mine), channel_id=1, source_target_pairs={{0,16},{16,0},{1,17},{17,1},{2,18},{18,2},{3,19},{19,3},{4,20},{20... | collective-permute-start | bytes 2654216 | tf_op jit(solution)/shard_map/ppermute | solution.py:355
  103.9 26.7 %collective-permute-start.25 = (bf16[1152,384]{1,0:T(8,128)(2,1)S(1)}, bf16[1152,384]{1,0:T(8,128)(2,1)S(1)}, u32[]{:S(2)}, u32[]{:S(2)}) collective-permute-start(bf16[1152,384]{1,0:T(8,128)(2,1)S(1)} %collective-permute-done.16.mine), channel_id=1, source_target_pairs={{0,16},{16,0},{1,17},{17,1},{2,18},{18,2},{3,19},{19,3},{4,20},{20... | collective-permute-start | bytes 2654216 | tf_op jit(solution)/shard_map/ppermute | solution.py:355
  122.7 12.2 %collective-permute-start.23 = (bf16[1152,384]{1,0:T(8,128)(2,1)S(1)}, bf16[1152,384]{1,0:T(8,128)(2,1)S(1)}, u32[]{:S(2)}, u32[]{:S(2)}) collective-permute-start(bf16[1152,384]{1,0:T(8,128)(2,1)S(1)} %shard_map.97.mine), channel_id=1, source_target_pairs={{0,16},{16,0},{1,17},{17,1},{2,18},{18,2},{3,19},{19,3},{4,20},{20... | collective-permute-start | bytes 2654216 | tf_op jit(solution)/shard_map/ppermute | solution.py:355
  122.9 14.0 %collective-permute-start.20 = (bf16[1152,384]{1,0:T(8,128)(2,1)S(1)}, bf16[1152,384]{1,0:T(8,128)(2,1)S(1)}, u32[]{:S(2)}, u32[]{:S(2)}) collective-permute-start(bf16[1152,384]{1,0:T(8,128)(2,1)S(1)} %shard_map.95.mine), channel_id=1, source_target_pairs={{0,16},{16,0},{1,17},{17,1},{2,18},{18,2},{3,19},{19,3},{4,20},{20... | collective-permute-start | bytes 2654216 | tf_op jit(solution)/shard_map/ppermute | solution.py:355
  (7 other events, 52.4 us)

commit v2 on v1

--- a/solution.py
+++ b/solution.py
@@ -122,12 +122,14 @@
     out[...] = read_counts(mine[rows:, :128]) + read_counts(theirs[rows:, :128])
 
 
-def pack_hidden(groups, most, hop, halves, table, hidden, *outs):
-    rows, top, inner = hidden.shape
-    width = inner // halves
+def pack_hidden(groups, most, hop, halves, table, hidden, *rest):
+    outs, held, sem = rest[:groups], rest[groups], rest[groups + 1]
+    rows, top, width = held.shape
     flat = rows * top
     part = other(lax.axis_index("dp"), hop, halves) if halves > 1 else 0
     columns = pl.ds(pl.multiple_of(part * width, 128), width)
+    copy = pltpu.make_async_copy(hidden.at[:, :, columns], held, sem)
+    copy.start()
     pad = table.shape[0] // 4
     key, routes = table[:pad], table[2 * pad : 3 * pad]
     spread = jnp.where(iota((rows, flat), 0) == iota((rows, flat), 1) // top, 1.0, 0.0).astype(BF16)
@@ -144,7 +146,8 @@
     label = other(me, iota((pad, flat), 0), groups).astype(F32)
     key = jnp.where(route == label, key, -1.0)
     slot = iota((most, flat), 0).astype(F32)
-    source = hidden[:, :, columns].reshape(flat, width)
+    copy.wait()
+    source = held[...].reshape(flat, width)
     for j in range(groups):
         at = jnp.where(slot == key[j : j + 1, :], 1.0, 0.0).astype(BF16)
         outs[j][...] = jnp.dot(at, source, preferred_element_type=F32).astype(BF16)
@@ -189,11 +192,25 @@
     return (m, m ^ 1, jnp.where(low, 2, 1), jnp.where(low, 3, 0))[step]
 
 
-def half_product(tile, ht, mine, out):
-    for i in range(0, ht.shape[0], tile):
-        out[i : i + tile, :] = jnp.dot(
-            ht[i : i + tile, :], mine[: ht.shape[1], :], preferred_element_type=F32
-        )
+def split(source, *outs):
+    at = 0
+    for out in outs:
+        out[...] = source[at : at + out.shape[0], :]
+        at += out.shape[0]
+
+
+def partial_product(tile, offsets, *refs):
+    out, pairs = refs[-1], refs[: 2 * len(offsets)]
+    earlier = refs[2 * len(offsets) : -1]
+    for i in range(0, out.shape[0], tile):
+        total = sum(x[i : i + tile, :] for x in earlier)
+        for k, offset in enumerate(offsets):
+            ht, x = pairs[2 * k : 2 * k + 2]
+            count = min(ht.shape[1] - offset, x.shape[0])
+            total += jnp.dot(
+                ht[i : i + tile, offset : offset + count], x[:count, :], preferred_element_type=F32
+            )
+        out[i : i + tile, :] = total
 
 
 def product(tile, line, steps, ht, *refs):
@@ -203,10 +220,12 @@
     rows = ht.shape[1]
     shard = out.shape[1] // line
     m = lax.axis_index("mp")
-    marks, at = [], 0
+    marks, at, spans = [], 0, []
     for step, x in zip(steps, theirs):
         width = x.shape[1]
-        joined[:, at : at + width] = x[:rows, :]
+        spans.append((rows - min(rows, x.shape[0]), at, at + width))
+        count_of = min(rows, x.shape[0])
+        joined[rows - count_of :, at : at + width] = x[:count_of, :]
         if step < 0:
             size = width // line
             marks += [(lax.rem(m + line - k, line) * shard, at + k * size, size) for k in range(line)]
@@ -215,12 +234,16 @@
         at += width
     copies = []
     for i in range(0, ht.shape[0], tile):
-        second = jnp.dot(ht[i : i + tile, :], joined[...], preferred_element_type=F32)
-        at = 0
-        for half in halves:
-            columns = slice(at, at + half.shape[1])
-            total[i : i + tile, columns] = half[i : i + tile, :] + second[:, columns]
-            at += half.shape[1]
+        if all(skip == 0 for skip, _, _ in spans):
+            both = jnp.dot(ht[i : i + tile, :], joined[...], preferred_element_type=F32)
+            second = [both[:, low:high] for _, low, high in spans]
+        else:
+            second = [
+                jnp.dot(ht[i : i + tile, skip:], joined[skip:, low:high], preferred_element_type=F32)
+                for skip, low, high in spans
+            ]
+        for half, rest, (_, low, high) in zip(halves, second, spans):
+            total[i : i + tile, low:high] = half[i : i + tile, :] + rest
         for k, (column, at, size) in enumerate(marks):
             copy = pltpu.make_async_copy(
                 total.at[pl.ds(i, tile), pl.ds(at, size)],
@@ -262,6 +285,8 @@
     rows = groups * most
     pad = 8 * (-(-groups // 8))
     operands = (routes.T, combine.T, block_pair, lengths, log_ratio, cotangent)
+    operands = tuple(pltpu.with_memory_space_constraint(x, pltpu.HBM) for x in operands)
+    hidden = pltpu.with_memory_space_constraint(hidden, pltpu.HBM)
 
     packed = call(
         functools.partial(pack_scaled, groups, most, early),
@@ -272,7 +297,7 @@
         ]
         + [jax.ShapeDtypeStruct((most, width), BF16)] * groups,
         [HBM] * 6,
-        60,
+        12,
         2 * groups * most * tokens * width,
         [pltpu.VMEM(x.shape, x.dtype) for x in operands] + [pltpu.SemaphoreType.DMA((6,))],
     )(*operands)
@@ -284,9 +309,10 @@
             functools.partial(pack_hidden, groups, most, h, halves),
             f"pack_hidden{h}",
             [jax.ShapeDtypeStruct((most, part), BF16)] * groups,
-            [VM, VM],
+            [VM, HBM],
             24,
             2 * rows * tokens * top * part,
+            [pltpu.VMEM((tokens, top, part), BF16), pltpu.SemaphoreType.DMA],
         )(table, hidden)
         for h in range(halves)
     ]
@@ -325,15 +351,21 @@
 
     pairs, middle, outward = [(0, 1), (1, 0), (2, 3), (3, 2)], [(1, 2), (2, 1)], [(1, 0), (2, 3)]
     p1, q1 = lax.ppermute(start, "mp", pairs), lax.ppermute(start, "mp", middle)
-    q2, p2 = lax.ppermute(p1, "mp", middle), lax.ppermute(q1, "mp", outward)
-    p3 = lax.ppermute(q2, "mp", outward)
+    cut = rows // 2
+    p1a, p1b = call(
+        split, "split", [jax.ShapeDtypeStruct((cut, width), BF16)] * 2, [VM], 8, 0
+    )(p1)
+    q2a, q2b = lax.ppermute(p1a, "mp", middle), lax.ppermute(p1b, "mp", middle)
+    p2 = lax.ppermute(q1, "mp", outward)
+    p3a, p3b = lax.ppermute(q2a, "mp", outward), lax.ppermute(q2b, "mp", outward)
 
     def picked(name, inner_rows, outer_rows):
-        return call(pick, name, jax.ShapeDtypeStruct((rows, width), BF16), [VM] * 2, 8, 0)(
+        return call(pick, name, jax.ShapeDtypeStruct(inner_rows.shape, BF16), [VM] * 2, 8, 0)(
             inner_rows, outer_rows
         )
 
-    shards = [start, p1, picked("pick2", q1, p2), picked("pick3", q2, p3)]
+    shards = [start, p1, picked("pick2", q1, p2)]
+    last_a, last_b = picked("pick_a", q2a, p3a), picked("pick_b", q2b, p3b)
 
     step = 128 if rows % 128 == 0 else most
     turned = [
@@ -354,15 +386,19 @@
     def swap(mine):
         return lax.ppermute(mine, "dp", [(0, 1), (1, 0)])
 
+    def accumulate(name, pairs, offsets, *earlier):
+        columns = pairs[0][1].shape[1]
+        return call(
+            functools.partial(partial_product, tile, offsets),
+            name,
+            jax.ShapeDtypeStruct((part, columns), F32),
+            [VM] * (2 * len(pairs) + len(earlier)),
+            16,
+            2 * part * cut * columns * len(pairs),
+        )(*[x for pair in pairs for x in pair], *earlier)
+
     def half(name, mine):
-        return call(
-            functools.partial(half_product, tile),
-            name,
-            jax.ShapeDtypeStruct((part, mine.shape[1]), F32),
-            [VM, VM],
-            12,
-            2 * part * rows * mine.shape[1],
-        )(turned[0], mine)
+        return accumulate(name, [(turned[0], mine)], (0,))
 
     def finish(name, halves, theirs, steps, out):
         columns = sum(x.shape[1] for x in theirs)
@@ -411,13 +447,10 @@
         0,
     )(*kept)
     other_core = swap(mine)
-    out = finish(
-        "last_product",
-        [half("half_early", mine), own[3]],
-        [other_core, theirs[3]],
-        (-1, 3),
-        out,
-    )
+    half_early = half("half_early", mine)
+    last = accumulate("half3a", [(turned[0], last_a), (turned[1], swap(last_a))], (0, 0))
+    last = accumulate("half3b", [(turned[0], last_b)], (cut,), last)
+    out = finish("last_product", [half_early, last], [other_core, swap(last_b)], (-1, 3), out)
     expert_load = call(
         functools.partial(tally, rows),
         "tally",

time: 141 us -> 126 us (0.89)
  waiting for transfers between devices: 83.7 us -> 60.5 us
  starting transfers between devices: 27.5 us -> 36.7 us
  local copies, waits for them, and re-layouts: 4.05 us -> 0.63 us
  Pallas kernels: 24.5 us -> 27 us
    ppermute x3, waiting for transfers between devices: 19.5 us -> 1.07 us  [work(): lax.ppermute(raw, 'mp', [(a, (a + k) % line) for a in range(line)])]
    ppermute x4, waiting for transfers between devices: 11.7 us -> 18.2 us  [work(): lax.ppermute(block, ('dp', 'expert'), [(a * groups + b, (a ^ h) * groups...]
    ppermute x3, waiting for transfers between devices: 10.3 us -> 4.85 us  [work(): lax.ppermute(scaled[j], 'expert', pairs_of(groups, j))]
    ppermute x4, starting transfers between devices: 0.29 us -> 5.57 us  [work(): lax.ppermute(block, ('dp', 'expert'), [(a * groups + b, (a ^ h) * groups...]
    unnamed x10 -> x0, local copies, waits for them, and re-layouts: 3.42 us -> none
    ppermute x3, waiting for transfers between devices: 14.1 us -> 10.9 us  [work(): lax.ppermute(sent[j], 'expert', pairs_of(groups, j))]
    ppermute x3, waiting for transfers between devices: 7.28 us -> 4.45 us  [work(): block = lax.ppermute(block, 'expert', pairs_of(groups, j))]
    pallas_call x2, Pallas kernels: 4.3 us -> 6.84 us  [work(): call(functools.partial(pack_hidden, groups, most, h, halves), f'pack_hidd...]
  transfers between devices with their start and end apart: 26 -> 29, of which waited for: 11 -> 10; matrix products, arithmetic and copies ran while one was open for 0% -> 0% of each run, Pallas kernels for 13% -> 17%
where the time goes in v2:
time: 126 us
  waiting for transfers between devices  60.5 us (48%)
  starting transfers between devices  36.7 us (29%)
  Pallas kernels  27 us (21%)
    ppermute x4, waiting for transfers between devices, work(): lax.ppermute(block, ('dp', 'expert'), [(a * groups + b, (a ^ h) * groups...  18.2 us
    ppermute x1, waiting for transfers between devices, work(): lax.ppermute(q2a, 'mp', outward)  14.6 us
    ppermute x3, waiting for transfers between devices, work(): lax.ppermute(sent[j], 'expert', pairs_of(groups, j))  10.9 us
    pallas_call x3, Pallas kernels, finish(): call(functools.partial(product, tile, line, steps), name, out_shape, [VM]...  8.07 us
    pallas_call x6, Pallas kernels, accumulate(): call(functools.partial(partial_product, tile, offsets), name, jax.ShapeDt...  7.64 us
    ppermute x3, starting transfers between devices, work(): lax.ppermute(raw, 'mp', [(a, (a + k) % line) for a in range(line)])  7.04 us
    pallas_call x2, Pallas kernels, work(): call(functools.partial(pack_hidden, groups, most, h, halves), f'pack_hidd...  6.84 us
    ppermute x1, waiting for transfers between devices, work(): lax.ppermute(q2b, 'mp', outward)  6.46 us
  transfers between devices with their start and end apart: 29, of which 10 were waited for; matrix products, arithmetic and copies ran while one was open for 0% of the time, Pallas kernels for 17%

profile of v2, /device:TPU:0, one launch (start us, length us, event | category | flops | bytes accessed | tf_op | source)
XLA Modules:
  0.0 126.0 jit_solution(4378401400102692198)
XLA Ops:
  0.6 1.9 %shard_map.86 = (f32[32,384]{1,0:T(8,128)S(1)}, bf16[384,128]{1,0:T(8,128)(2,1)S(1)}, bf16[288,384]{1,0:T(8,128)(2,1)S(1)}, bf16[288,384]{1,0:T(8,128)(2,1)S(1)}...) custom-call(s32[2,384]{1,0:T(2,128)} %bitcast.4, f32[2,384]{1,0:T(2,128)} %bitcast.5, s32[1,12]{1,0:T(1,128)} %refs_2_.1, ...), custom_call_target="tpu_custom_call" | custom-call | flops 339738624 | bytes 2015232 | tf_op jit(solution)/shard_map/pallas_call | solution.py:291
  2.5 3.1 %collective-permute-start.7 = (bf16[384,128]{1,0:T(8,128)(2,1)S(1)}, bf16[384,128]{1,0:T(8,128)(2,1)S(1)}, u32[]{:S(2)}, u32[]{:S(2)}) collective-permute-start(bf16[384,128]{1,0:T(8,128)(2,1)S(1)} %get-tuple-element.31.refs_0_), channel_id=1, source_target_pairs={{0,1},{1,2},{2,3},{3,0},{4,5},{5,6},{6,7},{7,4},{8,9},{9,10},{10,1... | collective-permute-start | bytes 294920 | tf_op jit(solution)/shard_map/ppermute | solution.py:427
  5.6 2.6 %collective-permute-start.8 = (bf16[384,128]{1,0:T(8,128)(2,1)S(1)}, bf16[384,128]{1,0:T(8,128)(2,1)S(1)}, u32[]{:S(2)}, u32[]{:S(2)}) collective-permute-start(bf16[384,128]{1,0:T(8,128)(2,1)S(1)} %get-tuple-element.31.refs_0_), channel_id=1, source_target_pairs={{0,2},{1,3},{2,0},{3,1},{4,6},{5,7},{6,4},{7,5},{8,10},{9,11},{10,... | collective-permute-start | bytes 294920 | tf_op jit(solution)/shard_map/ppermute | solution.py:427
  11.0 1.5 %collective-permute-start.14 = (bf16[288,384]{1,0:T(8,128)(2,1)S(1)}, bf16[288,384]{1,0:T(8,128)(2,1)S(1)}, u32[]{:S(2)}, u32[]{:S(2)}) collective-permute-start(bf16[288,384]{1,0:T(8,128)(2,1)S(1)} %get-tuple-element.38), channel_id=1, source_target_pairs={{0,8},{4,12},{8,0},{12,4},{1,9},{5,13},{9,1},{13,5},{2,10},{6,14},... | collective-permute-start | bytes 663560 | tf_op jit(solution)/shard_map/ppermute | solution.py:321
  15.6 1.6 %collective-permute-start.10 = (bf16[304,512]{1,0:T(8,128)(2,1)S(1)}, bf16[304,512]{1,0:T(8,128)(2,1)S(1)}, u32[]{:S(2)}, u32[]{:S(2)}) collective-permute-start(bf16[304,512]{1,0:T(8,128)(2,1)S(1)} %get-tuple-element.33), channel_id=1, source_target_pairs={{0,4},{4,0},{8,12},{12,8},{1,5},{5,1},{9,13},{13,9},{2,6},{6,2},{1... | collective-permute-start | bytes 933896 | tf_op jit(solution)/shard_map/ppermute | solution.py:439
  17.2 1.5 %collective-permute-start.11 = (bf16[304,512]{1,0:T(8,128)(2,1)S(1)}, bf16[304,512]{1,0:T(8,128)(2,1)S(1)}, u32[]{:S(2)}, u32[]{:S(2)}) collective-permute-start(bf16[304,512]{1,0:T(8,128)(2,1)S(1)} %get-tuple-element.34), channel_id=1, source_target_pairs={{0,8},{4,12},{8,0},{12,4},{1,9},{5,13},{9,1},{13,5},{2,10},{6,14},... | collective-permute-start | bytes 933896 | tf_op jit(solution)/shard_map/ppermute | solution.py:439
  18.7 2.7 %collective-permute-done.14.refs_2_ = bf16[288,384]{1,0:T(8,128)(2,1)S(1)} collective-permute-done((bf16[288,384]{1,0:T(8,128)(2,1)S(1)}, bf16[288,384]{1,0:T(8,128)(2,1)S(1)}, u32[]{:S(2)}, u32[]{:S(2)}) %collective-permute-start.14) | collective-permute-done | bytes 221216 | tf_op jit(solution)/shard_map/ppermute | solution.py:321
  21.4 2.1 %collective-permute-done.15.refs_3_ = bf16[288,384]{1,0:T(8,128)(2,1)S(1)} collective-permute-done((bf16[288,384]{1,0:T(8,128)(2,1)S(1)}, bf16[288,384]{1,0:T(8,128)(2,1)S(1)}, u32[]{:S(2)}, u32[]{:S(2)}) %collective-permute-start.15) | collective-permute-done | bytes 221216 | tf_op jit(solution)/shard_map/ppermute | solution.py:321
  24.4 3.4 %shard_map.89 = (bf16[288,896]{1,0:T(8,128)(2,1)S(1)}, bf16[288,896]{1,0:T(8,128)(2,1)S(1)}, bf16[288,896]{1,0:T(8,128)(2,1)S(1)}, bf16[288,896]{1,0:T(8,128)(2,1)S(1)}) custom-call(f32[32,384]{1,0:T(8,128)S(1)} %get-tuple-element.22.table, bf16[384,2,1792]{2,1,0:T(2,128)(2,1)} %hidden.3), custom_call_target="tpu_custom_call" | custom-call | flops 1585446912 | bytes 4128768 | tf_op jit(solution)/shard_map/pallas_call | solution.py:308
  27.8 1.6 %collective-permute-start.4 = (bf16[288,896]{1,0:T(8,128)(2,1)S(1)}, bf16[288,896]{1,0:T(8,128)(2,1)S(1)}, u32[]{:S(2)}, u32[]{:S(2)}) collective-permute-start(bf16[288,896]{1,0:T(8,128)(2,1)S(1)} %get-tuple-element.28), channel_id=1, source_target_pairs={{0,4},{4,0},{8,12},{12,8},{1,5},{5,1},{9,13},{13,9},{2,6},{6,2},{1... | collective-permute-start | bytes 1548296 | tf_op jit(solution)/shard_map/ppermute | solution.py:334
  31.4 3.9 %collective-permute-start.16 = (bf16[1152,384]{1,0:T(8,128)(2,1)S(1)}, bf16[1152,384]{1,0:T(8,128)(2,1)S(1)}, u32[]{:S(2)}, u32[]{:S(2)}) collective-permute-start(bf16[1152,384]{1,0:T(8,128)(2,1)S(1)} %shard_map.94.refs_1_), channel_id=1, source_target_pairs={{0,1},{1,0},{2,3},{3,2},{4,5},{5,4},{6,7},{7,6},{8,9},{9,8},{10,11... | collective-permute-start | bytes 2654216 | tf_op jit(solution)/shard_map/ppermute | solution.py:353
  35.2 10.9 %collective-permute-done.12.refs_3_ = bf16[304,512]{1,0:T(8,128)(2,1)S(1)} collective-permute-done((bf16[304,512]{1,0:T(8,128)(2,1)S(1)}, bf16[304,512]{1,0:T(8,128)(2,1)S(1)}, u32[]{:S(2)}, u32[]{:S(2)}) %collective-permute-start.12) | collective-permute-done | bytes 311328 | tf_op jit(solution)/shard_map/ppermute | solution.py:439
  46.1 2.3 %collective-permute-start.6 = (bf16[288,896]{1,0:T(8,128)(2,1)S(1)}, bf16[288,896]{1,0:T(8,128)(2,1)S(1)}, u32[]{:S(2)}, u32[]{:S(2)}) collective-permute-start(bf16[288,896]{1,0:T(8,128)(2,1)S(1)} %get-tuple-element.30), channel_id=1, source_target_pairs={{0,12},{4,8},{8,4},{12,0},{1,13},{5,9},{9,5},{13,1},{2,14},{6,10},... | collective-permute-start | bytes 1548296 | tf_op jit(solution)/shard_map/ppermute | solution.py:334
  48.4 3.4 %shard_map.87 = (bf16[288,896]{1,0:T(8,128)(2,1)S(1)}, bf16[288,896]{1,0:T(8,128)(2,1)S(1)}, bf16[288,896]{1,0:T(8,128)(2,1)S(1)}, bf16[288,896]{1,0:T(8,128)(2,1)S(1)}) custom-call(f32[32,384]{1,0:T(8,128)S(1)} %get-tuple-element.22.table, bf16[384,2,1792]{2,1,0:T(2,128)(2,1)} %hidden.3), custom_call_target="tpu_custom_call" | custom-call | flops 1585446912 | bytes 4128768 | tf_op jit(solution)/shard_map/pallas_call | solution.py:308
  51.9 4.4 %collective-permute-done.5.refs_2_ = bf16[288,896]{1,0:T(8,128)(2,1)S(1)} collective-permute-done((bf16[288,896]{1,0:T(8,128)(2,1)S(1)}, bf16[288,896]{1,0:T(8,128)(2,1)S(1)}, u32[]{:S(2)}, u32[]{:S(2)}) %collective-permute-start.5) | collective-permute-done | bytes 516128 | tf_op jit(solution)/shard_map/ppermute | solution.py:334
  57.6 3.3 %collective-permute-start.2 = (bf16[288,896]{1,0:T(8,128)(2,1)S(1)}, bf16[288,896]{1,0:T(8,128)(2,1)S(1)}, u32[]{:S(2)}, u32[]{:S(2)}) collective-permute-start(bf16[288,896]{1,0:T(8,128)(2,1)S(1)} %get-tuple-element.25), channel_id=1, source_target_pairs={{0,24},{4,28},{8,16},{12,20},{16,8},{20,12},{24,0},{28,4},{1,25},{... | collective-permute-start | bytes 1548296 | tf_op jit(solution)/shard_map/ppermute | solution.py:328
  61.9 8.1 %collective-permute-done.1.refs_1_ = bf16[288,896]{1,0:T(8,128)(2,1)S(1)} collective-permute-done((bf16[288,896]{1,0:T(8,128)(2,1)S(1)}, bf16[288,896]{1,0:T(8,128)(2,1)S(1)}, u32[]{:S(2)}, u32[]{:S(2)}) %collective-permute-start.1) | collective-permute-done | bytes 516128 | tf_op jit(solution)/shard_map/ppermute | solution.py:328
  69.9 2.2 %collective-permute-start.3 = (bf16[288,896]{1,0:T(8,128)(2,1)S(1)}, bf16[288,896]{1,0:T(8,128)(2,1)S(1)}, u32[]{:S(2)}, u32[]{:S(2)}) collective-permute-start(bf16[288,896]{1,0:T(8,128)(2,1)S(1)} %get-tuple-element.26), channel_id=1, source_target_pairs={{0,28},{4,24},{8,20},{12,16},{16,12},{20,8},{24,4},{28,0},{1,29},{... | collective-permute-start | bytes 1548296 | tf_op jit(solution)/shard_map/ppermute | solution.py:328
  75.0 9.2 %collective-permute-done.3.refs_3_ = bf16[288,896]{1,0:T(8,128)(2,1)S(1)} collective-permute-done((bf16[288,896]{1,0:T(8,128)(2,1)S(1)}, bf16[288,896]{1,0:T(8,128)(2,1)S(1)}, u32[]{:S(2)}, u32[]{:S(2)}) %collective-permute-start.3) | collective-permute-done | bytes 516128 | tf_op jit(solution)/shard_map/ppermute | solution.py:328
  85.4 14.6 %collective-permute-done.20.outer = bf16[576,384]{1,0:T(8,128)(2,1)S(1)} collective-permute-done((bf16[576,384]{1,0:T(8,128)(2,1)S(1)}, bf16[576,384]{1,0:T(8,128)(2,1)S(1)}, u32[]{:S(2)}, u32[]{:S(2)}) %collective-permute-start.20) | collective-permute-done | bytes 442400 | tf_op jit(solution)/shard_map/ppermute | solution.py:360
  106.8 6.5 %collective-permute-done.18.outer = bf16[576,384]{1,0:T(8,128)(2,1)S(1)} collective-permute-done((bf16[576,384]{1,0:T(8,128)(2,1)S(1)}, bf16[576,384]{1,0:T(8,128)(2,1)S(1)}, u32[]{:S(2)}, u32[]{:S(2)}) %collective-permute-start.18) | collective-permute-done | bytes 442400 | tf_op jit(solution)/shard_map/ppermute | solution.py:360
  115.3 2.9 %shard_map.104.refs_2_ = f32[896,2048]{1,0:T(8,128)} custom-call(bf16[896,1152]{1,0:T(8,128)(2,1)S(1)} %shard_map.88.refs_2_.ht, f32[896,384]{1,0:T(8,128)S(1)} %shard_map.102.refs_0_, f32[896,384]{1,0:T(8,128)S(1)} %shard_map.103.refs_1_, bf16[1152,384]{1,0:T(8,128)(2,1)S(1)} %collective-permute-done.27.refs_2_, ...), custom_call_target="tpu_custom_call" | custom-call | flops 1585446912 | bytes 7340032 | tf_op jit(solution)/shard_map/pallas_call | solution.py:407
  120.6 2.1 %shard_map.105.refs_4_ = f32[896,2048]{1,0:T(8,128)} custom-call(bf16[896,1152]{1,0:T(8,128)(2,1)S(1)} %shard_map.88.refs_2_.ht, f32[896,384]{1,0:T(8,128)S(1)} %shard_map.101.refs_0_, bf16[1152,384]{1,0:T(8,128)(2,1)S(1)} %collective-permute-done.26.refs_1_, f32[896,2048]{1,0:T(8,128)} %shard_map.104.refs_2_), custom_call_target="tpu_custom_call", output_to_operand_aliasing={{}: (3, {})} | custom-call | flops 792723456 | bytes 7340032 | tf_op jit(solution)/shard_map/pallas_call | solution.py:407
  122.7 3.1 %shard_map.106 = f32[896,2048]{1,0:T(8,128)} custom-call(bf16[896,1152]{1,0:T(8,128)(2,1)S(1)} %shard_map.88.refs_2_.ht, f32[896,512]{1,0:T(8,128)S(1)} %shard_map.93.refs_0_, f32[896,384]{1,0:T(8,128)S(1)} %shard_map.99.refs_1_, bf16[1168,512]{1,0:T(8,128)(2,1)S(1)} %collective-permute-done.22.refs_2_.theirs, ...), custom_call_target="tpu_custom_call", output_to_operand_aliasing={{}: (5, {})} | custom-call | flops 1849688064 | bytes 7340032 | tf_op jit(solution)/shard_map/pallas_call | solution.py:407
  (57 shorter events, 26.1 us)
Async XLA Ops:
  2.5 10.1 %collective-permute-start.7 = (bf16[384,128]{1,0:T(8,128)(2,1)S(1)}, bf16[384,128]{1,0:T(8,128)(2,1)S(1)}, u32[]{:S(2)}, u32[]{:S(2)}) collective-permute-start(bf16[384,128]{1,0:T(8,128)(2,1)S(1)} %get-tuple-element.31.refs_0_), channel_id=1, source_target_pairs={{0,1},{1,2},{2,3},{3,0},{4,5},{5,6},{6,7},{7,4},{8,9},{9,10},{10,1... | collective-permute-start | bytes 294920 | tf_op jit(solution)/shard_map/ppermute | solution.py:427
  11.0 10.4 %collective-permute-start.14 = (bf16[288,384]{1,0:T(8,128)(2,1)S(1)}, bf16[288,384]{1,0:T(8,128)(2,1)S(1)}, u32[]{:S(2)}, u32[]{:S(2)}) collective-permute-start(bf16[288,384]{1,0:T(8,128)(2,1)S(1)} %get-tuple-element.38), channel_id=1, source_target_pairs={{0,8},{4,12},{8,0},{12,4},{1,9},{5,13},{9,1},{13,5},{2,10},{6,14},... | collective-permute-start | bytes 663560 | tf_op jit(solution)/shard_map/ppermute | solution.py:321
  12.6 11.0 %collective-permute-start.15 = (bf16[288,384]{1,0:T(8,128)(2,1)S(1)}, bf16[288,384]{1,0:T(8,128)(2,1)S(1)}, u32[]{:S(2)}, u32[]{:S(2)}) collective-permute-start(bf16[288,384]{1,0:T(8,128)(2,1)S(1)} %get-tuple-element.39), channel_id=1, source_target_pairs={{0,12},{4,8},{8,4},{12,0},{1,13},{5,9},{9,5},{13,1},{2,14},{6,10},... | collective-permute-start | bytes 663560 | tf_op jit(solution)/shard_map/ppermute | solution.py:321
  15.6 14.4 %collective-permute-start.10 = (bf16[304,512]{1,0:T(8,128)(2,1)S(1)}, bf16[304,512]{1,0:T(8,128)(2,1)S(1)}, u32[]{:S(2)}, u32[]{:S(2)}) collective-permute-start(bf16[304,512]{1,0:T(8,128)(2,1)S(1)} %get-tuple-element.33), channel_id=1, source_target_pairs={{0,4},{4,0},{8,12},{12,8},{1,5},{5,1},{9,13},{13,9},{2,6},{6,2},{1... | collective-permute-start | bytes 933896 | tf_op jit(solution)/shard_map/ppermute | solution.py:439
  17.2 14.2 %collective-permute-start.11 = (bf16[304,512]{1,0:T(8,128)(2,1)S(1)}, bf16[304,512]{1,0:T(8,128)(2,1)S(1)}, u32[]{:S(2)}, u32[]{:S(2)}) collective-permute-start(bf16[304,512]{1,0:T(8,128)(2,1)S(1)} %get-tuple-element.34), channel_id=1, source_target_pairs={{0,8},{4,12},{8,0},{12,4},{1,9},{5,13},{9,1},{13,5},{2,10},{6,14},... | collective-permute-start | bytes 933896 | tf_op jit(solution)/shard_map/ppermute | solution.py:439
  23.6 32.7 %collective-permute-start.24 = (bf16[1152,384]{1,0:T(8,128)(2,1)S(1)}, bf16[1152,384]{1,0:T(8,128)(2,1)S(1)}, u32[]{:S(2)}, u32[]{:S(2)}) collective-permute-start(bf16[1152,384]{1,0:T(8,128)(2,1)S(1)} %shard_map.94.refs_1_), channel_id=1, source_target_pairs={{1,2},{2,1},{5,6},{6,5},{9,10},{10,9},{13,14},{14,13},{17,18},{18,... | collective-permute-start | bytes 2654216 | tf_op jit(solution)/shard_map/ppermute | solution.py:353
  27.8 24.0 %collective-permute-start.4 = (bf16[288,896]{1,0:T(8,128)(2,1)S(1)}, bf16[288,896]{1,0:T(8,128)(2,1)S(1)}, u32[]{:S(2)}, u32[]{:S(2)}) collective-permute-start(bf16[288,896]{1,0:T(8,128)(2,1)S(1)} %get-tuple-element.28), channel_id=1, source_target_pairs={{0,4},{4,0},{8,12},{12,8},{1,5},{5,1},{9,13},{13,9},{2,6},{6,2},{1... | collective-permute-start | bytes 1548296 | tf_op jit(solution)/shard_map/ppermute | solution.py:334
  29.3 16.7 %collective-permute-start.12 = (bf16[304,512]{1,0:T(8,128)(2,1)S(1)}, bf16[304,512]{1,0:T(8,128)(2,1)S(1)}, u32[]{:S(2)}, u32[]{:S(2)}) collective-permute-start(bf16[304,512]{1,0:T(8,128)(2,1)S(1)} %get-tuple-element.35), channel_id=1, source_target_pairs={{0,12},{4,8},{8,4},{12,0},{1,13},{5,9},{9,5},{13,1},{2,14},{6,10},... | collective-permute-start | bytes 933896 | tf_op jit(solution)/shard_map/ppermute | solution.py:439
  30.0 26.3 %collective-permute-start.5 = (bf16[288,896]{1,0:T(8,128)(2,1)S(1)}, bf16[288,896]{1,0:T(8,128)(2,1)S(1)}, u32[]{:S(2)}, u32[]{:S(2)}) collective-permute-start(bf16[288,896]{1,0:T(8,128)(2,1)S(1)} %get-tuple-element.29), channel_id=1, source_target_pairs={{0,8},{4,12},{8,0},{12,4},{1,9},{5,13},{9,1},{13,5},{2,10},{6,14},... | collective-permute-start | bytes 1548296 | tf_op jit(solution)/shard_map/ppermute | solution.py:334
  31.4 29.6 %collective-permute-start.16 = (bf16[1152,384]{1,0:T(8,128)(2,1)S(1)}, bf16[1152,384]{1,0:T(8,128)(2,1)S(1)}, u32[]{:S(2)}, u32[]{:S(2)}) collective-permute-start(bf16[1152,384]{1,0:T(8,128)(2,1)S(1)} %shard_map.94.refs_1_), channel_id=1, source_target_pairs={{0,1},{1,0},{2,3},{3,2},{4,5},{5,4},{6,7},{7,6},{8,9},{9,8},{10,11... | collective-permute-start | bytes 2654216 | tf_op jit(solution)/shard_map/ppermute | solution.py:353
  46.1 11.6 %collective-permute-start.6 = (bf16[288,896]{1,0:T(8,128)(2,1)S(1)}, bf16[288,896]{1,0:T(8,128)(2,1)S(1)}, u32[]{:S(2)}, u32[]{:S(2)}) collective-permute-start(bf16[288,896]{1,0:T(8,128)(2,1)S(1)} %get-tuple-element.30), channel_id=1, source_target_pairs={{0,12},{4,8},{8,4},{12,0},{1,13},{5,9},{9,5},{13,1},{2,14},{6,10},... | collective-permute-start | bytes 1548296 | tf_op jit(solution)/shard_map/ppermute | solution.py:334
  56.3 13.6 %collective-permute-start.1 = (bf16[288,896]{1,0:T(8,128)(2,1)S(1)}, bf16[288,896]{1,0:T(8,128)(2,1)S(1)}, u32[]{:S(2)}, u32[]{:S(2)}) collective-permute-start(bf16[288,896]{1,0:T(8,128)(2,1)S(1)} %get-tuple-element.24), channel_id=1, source_target_pairs={{0,20},{4,16},{8,28},{12,24},{16,4},{20,0},{24,12},{28,8},{1,21},{... | collective-permute-start | bytes 1548296 | tf_op jit(solution)/shard_map/ppermute | solution.py:328
  56.3 28.4 %collective-permute-start.25 = (bf16[1152,384]{1,0:T(8,128)(2,1)S(1)}, bf16[1152,384]{1,0:T(8,128)(2,1)S(1)}, u32[]{:S(2)}, u32[]{:S(2)}) collective-permute-start(bf16[1152,384]{1,0:T(8,128)(2,1)S(1)} %collective-permute-done.24.inner), channel_id=1, source_target_pairs={{1,0},{2,3},{5,4},{6,7},{9,8},{10,11},{13,12},{14,15},{17,16},{18,... | collective-permute-start | bytes 2654216 | tf_op jit(solution)/shard_map/ppermute | solution.py:359
  57.6 15.4 %collective-permute-start.2 = (bf16[288,896]{1,0:T(8,128)(2,1)S(1)}, bf16[288,896]{1,0:T(8,128)(2,1)S(1)}, u32[]{:S(2)}, u32[]{:S(2)}) collective-permute-start(bf16[288,896]{1,0:T(8,128)(2,1)S(1)} %get-tuple-element.25), channel_id=1, source_target_pairs={{0,24},{4,28},{8,16},{12,20},{16,8},{20,12},{24,0},{28,4},{1,25},{... | collective-permute-start | bytes 1548296 | tf_op jit(solution)/shard_map/ppermute | solution.py:328
  61.0 41.1 %collective-permute-start.22 = (bf16[1168,512]{1,0:T(8,128)(2,1)S(1)}, bf16[1168,512]{1,0:T(8,128)(2,1)S(1)}, u32[]{:S(2)}, u32[]{:S(2)}) collective-permute-start(bf16[1168,512]{1,0:T(8,128)(2,1)S(1)} %shard_map.92.refs_1_.mine), channel_id=1, source_target_pairs={{0,16},{16,0},{1,17},{17,1},{2,18},{18,2},{3,19},{19,3},{4,20},{20... | collective-permute-start | bytes 3588104 | tf_op jit(solution)/shard_map/ppermute | solution.py:387
  61.2 12.6 %collective-permute-start.19 = (bf16[576,384]{1,0:T(8,128)(2,1)S(1)}, bf16[576,384]{1,0:T(8,128)(2,1)S(1)}, u32[]{:S(2)}, u32[]{:S(2)}) collective-permute-start(bf16[576,384]{1,0:T(8,128)(2,1)S(1)} %get-tuple-element.41), channel_id=1, source_target_pairs={{1,2},{2,1},{5,6},{6,5},{9,10},{10,9},{13,14},{14,13},{17,18},{18,... | collective-permute-start | bytes 1327112 | tf_op jit(solution)/shard_map/ppermute | solution.py:358
  69.9 14.4 %collective-permute-start.3 = (bf16[288,896]{1,0:T(8,128)(2,1)S(1)}, bf16[288,896]{1,0:T(8,128)(2,1)S(1)}, u32[]{:S(2)}, u32[]{:S(2)}) collective-permute-start(bf16[288,896]{1,0:T(8,128)(2,1)S(1)} %get-tuple-element.26), channel_id=1, source_target_pairs={{0,28},{4,24},{8,20},{12,16},{16,12},{20,8},{24,4},{28,0},{1,29},{... | collective-permute-start | bytes 1548296 | tf_op jit(solution)/shard_map/ppermute | solution.py:328
  73.0 11.8 %collective-permute-start.17 = (bf16[576,384]{1,0:T(8,128)(2,1)S(1)}, bf16[576,384]{1,0:T(8,128)(2,1)S(1)}, u32[]{:S(2)}, u32[]{:S(2)}) collective-permute-start(bf16[576,384]{1,0:T(8,128)(2,1)S(1)} %get-tuple-element.40), channel_id=1, source_target_pairs={{1,2},{2,1},{5,6},{6,5},{9,10},{10,9},{13,14},{14,13},{17,18},{18,... | collective-permute-start | bytes 1327112 | tf_op jit(solution)/shard_map/ppermute | solution.py:358
  73.7 26.2 %collective-permute-start.20 = (bf16[576,384]{1,0:T(8,128)(2,1)S(1)}, bf16[576,384]{1,0:T(8,128)(2,1)S(1)}, u32[]{:S(2)}, u32[]{:S(2)}) collective-permute-start(bf16[576,384]{1,0:T(8,128)(2,1)S(1)} %collective-permute-done.19.inner), channel_id=1, source_target_pairs={{1,0},{2,3},{5,4},{6,7},{9,8},{10,11},{13,12},{14,15},{17,16},{18,... | collective-permute-start | bytes 1327112 | tf_op jit(solution)/shard_map/ppermute | solution.py:360
  84.3 31.0 %collective-permute-start.27 = (bf16[1152,384]{1,0:T(8,128)(2,1)S(1)}, bf16[1152,384]{1,0:T(8,128)(2,1)S(1)}, u32[]{:S(2)}, u32[]{:S(2)}) collective-permute-start(bf16[1152,384]{1,0:T(8,128)(2,1)S(1)} %shard_map.94.refs_1_), channel_id=1, source_target_pairs={{0,16},{16,0},{1,17},{17,1},{2,18},{18,2},{3,19},{19,3},{4,20},{20... | collective-permute-start | bytes 2654216 | tf_op jit(solution)/shard_map/ppermute | solution.py:387
  84.7 30.6 %collective-permute-start.28 = (bf16[1152,384]{1,0:T(8,128)(2,1)S(1)}, bf16[1152,384]{1,0:T(8,128)(2,1)S(1)}, u32[]{:S(2)}, u32[]{:S(2)}) collective-permute-start(bf16[1152,384]{1,0:T(8,128)(2,1)S(1)} %collective-permute-done.16.source.refs_1_), channel_id=1, source_target_pairs={{0,16},{16,0},{1,17},{17,1},{2,18},{18,2},{3,19},{19,3},{4,20},{20... | collective-permute-start | bytes 2654216 | tf_op jit(solution)/shard_map/ppermute | solution.py:387
  84.9 35.7 %collective-permute-start.26 = (bf16[1152,384]{1,0:T(8,128)(2,1)S(1)}, bf16[1152,384]{1,0:T(8,128)(2,1)S(1)}, u32[]{:S(2)}, u32[]{:S(2)}) collective-permute-start(bf16[1152,384]{1,0:T(8,128)(2,1)S(1)} %shard_map.100.refs_1_), channel_id=1, source_target_pairs={{0,16},{16,0},{1,17},{17,1},{2,18},{18,2},{3,19},{19,3},{4,20},{20... | collective-permute-start | bytes 2654216 | tf_op jit(solution)/shard_map/ppermute | solution.py:387
  100.0 13.3 %collective-permute-start.18 = (bf16[576,384]{1,0:T(8,128)(2,1)S(1)}, bf16[576,384]{1,0:T(8,128)(2,1)S(1)}, u32[]{:S(2)}, u32[]{:S(2)}) collective-permute-start(bf16[576,384]{1,0:T(8,128)(2,1)S(1)} %collective-permute-done.17.inner), channel_id=1, source_target_pairs={{1,0},{2,3},{5,4},{6,7},{9,8},{10,11},{13,12},{14,15},{17,16},{18,... | collective-permute-start | bytes 1327112 | tf_op jit(solution)/shard_map/ppermute | solution.py:360
  102.1 16.1 %collective-permute-start.21 = (bf16[576,384]{1,0:T(8,128)(2,1)S(1)}, bf16[576,384]{1,0:T(8,128)(2,1)S(1)}, u32[]{:S(2)}, u32[]{:S(2)}) collective-permute-start(bf16[576,384]{1,0:T(8,128)(2,1)S(1)} %shard_map.97.refs_1_), channel_id=1, source_target_pairs={{0,16},{16,0},{1,17},{17,1},{2,18},{18,2},{3,19},{19,3},{4,20},{20... | collective-permute-start | bytes 1327112 | tf_op jit(solution)/shard_map/ppermute | solution.py:387
  (5 other events, 43.8 us)
